TPU v7x, 32 devices: a whole 2x2x4 slice. The times are simulated.
32 devices in a mesh: seq: 2 (over core), fsdp: 16 (over z, y, x).
Axes of the slice: x: 2, y: 2, z: 4, core: 2. Of those that a mesh axis runs over, the one named last changes fastest.
Arguments:
- token_ids: int32 [2, 16, 1024], P(None, 'fsdp', 'seq'), may hold values from 0 to 31999
- lengths: int32 [2, 16], P(None, 'fsdp'), may hold values from 256 to 1024, as said below
- loss_positions: int32 [2, 16, 32], P(None, 'fsdp', 'seq'), may hold values from 0 to 511, as said below
- loss_targets: int32 [2, 16, 32], P(None, 'fsdp', 'seq'), may hold values from 0 to 31999
- attention_in: float32 [1, 768, 2316], P(None, ('seq', 'fsdp'))
- attention_in_moment: float32 [1, 768, 2316], P(None, ('seq', 'fsdp')), may hold values from -0.00010681152 to 0.00010681152
- attention_in_average: float32 [1, 768, 2316], P(None, ('seq', 'fsdp')), may hold values from -0.21875 to 0.21875
- attention_out: float32 [1, 768, 768], P(None, ('seq', 'fsdp')), may hold values from -0.875 to 0.875
- attention_out_moment: float32 [1, 768, 768], P(None, ('seq', 'fsdp')), may hold values from -0.00010681152 to 0.00010681152
- attention_out_average: float32 [1, 768, 768], P(None, ('seq', 'fsdp')), may hold values from -0.875 to 0.875
- feed_in: float32 [1, 768, 4096], P(None, ('seq', 'fsdp')), may hold values from -0.21875 to 0.21875
- feed_in_moment: float32 [1, 768, 4096], P(None, ('seq', 'fsdp')), may hold values from -0.00010681152 to 0.00010681152
- feed_in_average: float32 [1, 768, 4096], P(None, ('seq', 'fsdp')), may hold values from -0.21875 to 0.21875
- feed_out: float32 [1, 2048, 768], P(None, ('seq', 'fsdp')), may hold values from -0.125 to 0.125
- feed_out_moment: float32 [1, 2048, 768], P(None, ('seq', 'fsdp')), may hold values from -0.00010681152 to 0.00010681152
- feed_out_average: float32 [1, 2048, 768], P(None, ('seq', 'fsdp')), may hold values from -0.125 to 0.125
- embedding: float32 [32000, 768], P(None, ('seq', 'fsdp'))
- embedding_moment: float32 [32000, 768], P(None, ('seq', 'fsdp')), may hold values from -0.00010681152 to 0.00010681152
- embedding_average: float32 [32000, 768], P(None, ('seq', 'fsdp')), may hold values from -6 to 6
- unembedding: float32 [32000, 768], P(('seq', 'fsdp'))
- unembedding_moment: float32 [32000, 768], P(('seq', 'fsdp')), may hold values from -0.00010681152 to 0.00010681152
- unembedding_average: float32 [32000, 768], P(('seq', 'fsdp')), may hold values from -0.4375 to 0.4375
- gains_biases: float32 [2316], replicated
- gains_biases_moment: float32 [2316], replicated, may hold values from -0.0009765625 to 0.0009765625
- gains_biases_average: float32 [2316], replicated, may hold values from -6 to 6
Outputs:
- loss_value: float32 [], replicated
- grad_norm: float32 [], replicated
- attention_in_new: float32 [1, 768, 2316], P(None, ('seq', 'fsdp'))
- attention_in_moment_new: float32 [1, 768, 2316], P(None, ('seq', 'fsdp'))
- attention_in_average_new: float32 [1, 768, 2316], P(None, ('seq', 'fsdp'))
- attention_out_new: float32 [1, 768, 768], P(None, ('seq', 'fsdp'))
- attention_out_moment_new: float32 [1, 768, 768], P(None, ('seq', 'fsdp'))
- attention_out_average_new: float32 [1, 768, 768], P(None, ('seq', 'fsdp'))
- feed_in_new: float32 [1, 768, 4096], P(None, ('seq', 'fsdp'))
- feed_in_moment_new: float32 [1, 768, 4096], P(None, ('seq', 'fsdp'))
- feed_in_average_new: float32 [1, 768, 4096], P(None, ('seq', 'fsdp'))
- feed_out_new: float32 [1, 2048, 768], P(None, ('seq', 'fsdp'))
- feed_out_moment_new: float32 [1, 2048, 768], P(None, ('seq', 'fsdp'))
- feed_out_average_new: float32 [1, 2048, 768], P(None, ('seq', 'fsdp'))
- embedding_new: float32 [32000, 768], P(None, ('seq', 'fsdp'))
- embedding_moment_new: float32 [32000, 768], P(None, ('seq', 'fsdp'))
- embedding_average_new: float32 [32000, 768], P(None, ('seq', 'fsdp'))
- unembedding_new: float32 [32000, 768], P(('seq', 'fsdp'))
- unembedding_moment_new: float32 [32000, 768], P(('seq', 'fsdp'))
- unembedding_average_new: float32 [32000, 768], P(('seq', 'fsdp'))
- gains_biases_new: float32 [2316], replicated
- gains_biases_moment_new: float32 [2316], replicated
- gains_biases_average_new: float32 [2316], replicated
Inputs may be any that keep to these rules, and one draw needn't show every extreme that they name: Each slot holds one sequence of lengths[m, g] tokens at its start, the rest is padding; in each micro-batch one slot is full and another holds 256 tokens. `loss_positions`: column c names a token of the part c // 16 of the slot, counted from that part's start; the 16 positions of one part rise strictly.
All inputs are finite; a program needn't handle non-finite values.
Results may differ from a plain program's by a relative error of at most 0.0025.
The roundings to bfloat16 on the way count: a program that leaves them out, or rounds other values in their place, can miss the bound.
Values may be sent and summed in bfloat16 or wider, within the bound.
A program may use at most 256 MiB of HBM per device.

v0:
```python
import jax
import jax.numpy as jnp
from jax import lax
from jax.sharding import PartitionSpec as P

D = 768
H = 12
HD = 64
FF = 2048
V = 32000


epsilon = 1e-06
smooth = 0.1
z_weight = 0.005
clip_limit = 0.5
moment = 0.9
average = 0.9
rate_layer = 200.0
rate_head = 1000.0
rate_embed = 5000.0
block_rows = 512
negative = -1e30


def merged(array, axis, join):
    gathered = jax.tree.map(
        lambda a, kind: lax.all_gather(a.astype(kind), axis),
        array,
        (jnp.bfloat16, jnp.bfloat16, jnp.bfloat16, jnp.bfloat16),
    )

    def take(source):
        return jax.tree.map(
            lambda a, own: lax.dynamic_index_in_dim(a, source, 0, False).astype(own.dtype),
            gathered,
            array,
        )

    return lax.fori_loop(
        1, lax.axis_size(axis), lambda source, state: join(state, take(source)), take(0)
    )


def matmul(left_side, right_side):
    return jnp.dot(left_side, right_side, preferred_element_type=jnp.float32)


def cross_left(left_side, right_side):
    return lax.dot_general(
        left_side, right_side, (((0,), (0,)), ((), ())), preferred_element_type=jnp.float32
    )


def cross_right(left_side, right_side):
    return lax.dot_general(
        left_side, right_side, (((1,), (1,)), ((), ())), preferred_element_type=jnp.float32
    )


def norm_forward(values, gain_row):
    inverse = lax.rsqrt(jnp.mean(values * values, axis=-1, keepdims=True) + epsilon)
    return (values * inverse * gain_row, inverse)


def norm_backward(values, inverse, gain_row, grad_out):
    scaled = grad_out * gain_row
    grad_gain = jnp.sum(grad_out * values * inverse, axis=0)
    grad_in = inverse * scaled - values * inverse**3 * jnp.mean(
        values * scaled, axis=-1, keepdims=True
    )
    return (grad_in, grad_gain)


def split_heads(heads_part):
    length_all = heads_part.shape[0]
    heads_here = heads_part.shape[2] // HD
    return tuple(
        (heads_part[:, index_part].reshape(length_all, heads_here, HD) for index_part in range(3))
    )


def block_scores(query_block, key_rows, decay_sum, row_start, row_count):
    raw_scores = jnp.einsum(
        "ihd,jhd->hij", query_block, key_rows, preferred_element_type=jnp.float32
    ) * HD ** (-0.5)
    row_decay = lax.dynamic_slice_in_dim(decay_sum, row_start, row_count, 1)
    scores = raw_scores + row_decay[:, :, None] - decay_sum[:, None, :]
    rows_at = row_start + jnp.arange(row_count)
    causal = rows_at[:, None] >= jnp.arange(key_rows.shape[0])[None, :]
    return jnp.where(causal[None], scores, negative)


def attend(query_rows, key_rows, value_rows, decay_sum):
    length_all, heads_here, head_size = query_rows.shape
    step_rows = min(block_rows, length_all)
    starts = jnp.arange(length_all // step_rows) * step_rows

    def one_block(row_start):
        query_block = lax.dynamic_slice_in_dim(query_rows, row_start, step_rows, 0)
        scores = block_scores(query_block, key_rows, decay_sum, row_start, step_rows)
        row_peak = jnp.max(scores, axis=-1, keepdims=True)
        log_total = row_peak + jnp.log(jnp.sum(jnp.exp(scores - row_peak), axis=-1, keepdims=True))
        attention = jnp.exp(scores - log_total).astype(jnp.bfloat16)
        mixed_heads = jnp.einsum(
            "hij,jhd->ihd", attention, value_rows, preferred_element_type=jnp.float32
        )
        return (mixed_heads, log_total[:, :, 0])

    mixed_heads, log_total = lax.map(one_block, starts)
    mixed_heads = mixed_heads.reshape(length_all, heads_here, head_size)
    log_total = jnp.transpose(log_total, (1, 0, 2)).reshape(heads_here, length_all)
    return (mixed_heads, log_total)


def attend_back(query_rows, key_rows, value_rows, decay_sum, log_total, grad_mixed):
    length_all, heads_here, head_size = query_rows.shape
    step_rows = min(block_rows, length_all)
    starts = jnp.arange(length_all // step_rows) * step_rows

    def one_block(running, row_start):
        grad_keys, grad_values, decay_cols = running
        query_block = lax.dynamic_slice_in_dim(query_rows, row_start, step_rows, 0)
        grad_block = lax.dynamic_slice_in_dim(grad_mixed, row_start, step_rows, 0)
        scores = block_scores(query_block, key_rows, decay_sum, row_start, step_rows)
        totals = lax.dynamic_slice_in_dim(log_total, row_start, step_rows, 1)
        attention = jnp.exp(scores - totals[:, :, None])
        grad_attention = jnp.einsum(
            "ihd,jhd->hij", grad_block, value_rows, preferred_element_type=jnp.float32
        )
        inner_sum = jnp.sum(attention * grad_attention, axis=-1, keepdims=True)
        grad_scores = (attention * (grad_attention - inner_sum)).astype(jnp.bfloat16)
        grad_query = jnp.einsum(
            "hij,jhd->ihd", grad_scores, key_rows, preferred_element_type=jnp.float32
        ) * HD ** (-0.5)
        grad_keys = grad_keys + jnp.einsum(
            "hij,ihd->jhd", grad_scores, query_block, preferred_element_type=jnp.float32
        ) * HD ** (-0.5)
        grad_values = grad_values + jnp.einsum(
            "hij,ihd->jhd",
            attention.astype(jnp.bfloat16),
            grad_block,
            preferred_element_type=jnp.float32,
        )
        score_grads = grad_scores.astype(jnp.float32)
        decay_rows = jnp.sum(score_grads, axis=-1)
        decay_cols = decay_cols + jnp.sum(score_grads, axis=1)
        return ((grad_keys, grad_values, decay_cols), (grad_query, decay_rows))

    initial = (
        jnp.zeros((length_all, heads_here, head_size), jnp.float32),
        jnp.zeros((length_all, heads_here, head_size), jnp.float32),
        jnp.zeros((heads_here, length_all), jnp.float32),
    )
    (grad_keys, grad_values, decay_cols), (grad_query, decay_rows) = lax.scan(
        one_block, initial, starts
    )
    grad_query = grad_query.reshape(length_all, heads_here, head_size)
    decay_rows = jnp.transpose(decay_rows, (1, 0, 2)).reshape(heads_here, length_all)
    return (grad_query, grad_keys, grad_values, decay_rows - decay_cols)


def layer_forward(residual, weights, gain_one, gain_two, bias_row):
    weight_in, weight_out, feed_weight, down_weight = weights
    half_rows = residual.shape[0]
    normed_one, inverse_one = norm_forward(residual, gain_one)
    normed_one = normed_one.astype(jnp.bfloat16)
    project = matmul(normed_one, weight_in)
    heads_part = project[:, : 3 * D].astype(jnp.bfloat16).reshape(half_rows, 3, D)
    forget_part = (project[:, 3 * D :] + bias_row).astype(jnp.bfloat16).reshape(half_rows, 1, H)
    heads_part, forget_part = (
        lax.all_to_all(heads_part, "seq", split_axis=2, concat_axis=0, tiled=True),
        lax.all_to_all(forget_part, "seq", split_axis=2, concat_axis=0, tiled=True),
    )
    query_rows, key_rows, value_rows = split_heads(heads_part)
    forget_wide = forget_part[:, 0].astype(jnp.float32)
    decay_sum = jnp.cumsum(jax.nn.log_sigmoid(forget_wide), axis=0).T
    mixed_heads, log_total = attend(query_rows, key_rows, value_rows, decay_sum)
    mixed_low = mixed_heads.reshape(heads_part.shape[0], heads_part.shape[2]).astype(jnp.bfloat16)
    mixed_rows = lax.all_to_all(mixed_low, "seq", split_axis=0, concat_axis=1, tiled=True)
    middle = residual + matmul(mixed_rows, weight_out)
    normed_two, inverse_two = norm_forward(middle, gain_two)
    normed_two = normed_two.astype(jnp.bfloat16)
    gate_up = matmul(normed_two, feed_weight)
    hidden = (jax.nn.silu(gate_up[:, :FF]) * gate_up[:, FF:]).astype(jnp.bfloat16)
    result = middle + matmul(hidden, down_weight)
    kept_values = (
        residual,
        inverse_one,
        normed_one,
        heads_part,
        forget_wide,
        decay_sum,
        log_total,
        mixed_rows,
        middle,
        inverse_two,
        normed_two,
        gate_up,
        hidden,
    )
    return (result, kept_values)


def layer_backward(grad_resid, weights, gain_one, gain_two, kept_values):
    weight_in, weight_out, feed_weight, down_weight = weights
    (
        residual,
        inverse_one,
        normed_one,
        heads_part,
        forget_wide,
        decay_sum,
        log_total,
        mixed_rows,
        middle,
        inverse_two,
        normed_two,
        gate_up,
        hidden,
    ) = kept_values
    half_rows = residual.shape[0]
    grad_branch = grad_resid.astype(jnp.bfloat16)
    grad_down = cross_left(hidden, grad_branch)
    grad_hidden = cross_right(grad_branch, down_weight)
    gate_half = gate_up[:, :FF]
    up_half = gate_up[:, FF:]
    gate_sigmoid = jax.nn.sigmoid(gate_half)
    grad_gate = grad_hidden * up_half * gate_sigmoid * (1.0 + gate_half * (1.0 - gate_sigmoid))
    grad_up = grad_hidden * gate_half * gate_sigmoid
    grad_gate_up = jnp.concatenate([grad_gate, grad_up], axis=1).astype(jnp.bfloat16)
    grad_feed = cross_left(normed_two, grad_gate_up)
    grad_normed = cross_right(grad_gate_up, feed_weight)
    grad_two, gain_grad_two = norm_backward(middle, inverse_two, gain_two, grad_normed)
    grad_middle = grad_resid + grad_two
    grad_branch = grad_middle.astype(jnp.bfloat16)
    grad_out = cross_left(mixed_rows, grad_branch)
    grad_mixed = cross_right(grad_branch, weight_out).astype(jnp.bfloat16)
    grad_heads = lax.all_to_all(grad_mixed, "seq", split_axis=1, concat_axis=0, tiled=True)
    query_rows, key_rows, value_rows = split_heads(heads_part)
    length_all, heads_here, head_size = query_rows.shape
    grad_query, grad_keys, grad_values, grad_decay = attend_back(
        query_rows,
        key_rows,
        value_rows,
        decay_sum,
        log_total,
        grad_heads.reshape(length_all, heads_here, head_size),
    )
    grad_logf = lax.cumsum(grad_decay, axis=1, reverse=True).T
    grad_forget = (
        (grad_logf * jax.nn.sigmoid(-forget_wide))
        .astype(jnp.bfloat16)
        .reshape(length_all, 1, heads_here)
    )
    grad_parts = (
        jnp.stack([grad_query, grad_keys, grad_values], axis=1)
        .reshape(length_all, 3, heads_here * head_size)
        .astype(jnp.bfloat16)
    )
    grad_parts, grad_forget = (
        lax.all_to_all(grad_parts, "seq", split_axis=0, concat_axis=2, tiled=True),
        lax.all_to_all(grad_forget, "seq", split_axis=0, concat_axis=2, tiled=True),
    )
    grad_forget = grad_forget.reshape(half_rows, H)
    grad_project = jnp.concatenate([grad_parts.reshape(half_rows, 3 * D), grad_forget], axis=1)
    grad_weight_in = cross_left(normed_one, grad_project)
    grad_bias = jnp.sum(grad_forget.astype(jnp.float32), axis=0)
    grad_normed = cross_right(grad_project, weight_in)
    grad_one, gain_grad_one = norm_backward(residual, inverse_one, gain_one, grad_normed)
    return (
        grad_middle + grad_one,
        (grad_weight_in, grad_out, grad_feed, grad_down),
        (gain_grad_one, gain_grad_two, grad_bias),
    )


def combine_stats(first, second):
    row_top = jnp.maximum(first[0], second[0])
    spread = first[1] * jnp.exp(first[0] - row_top) + second[1] * jnp.exp(second[0] - row_top)
    return (row_top, spread, first[2] + second[2], first[3] + second[3])


def apply_update(weight_old, grad_full, moment_old, average_old, factor, rate):
    clipped = factor * grad_full
    moment_new = moment * moment_old + clipped
    weight_new = weight_old - rate * (clipped + moment * moment_new)
    average_new = average * average_old + (1.0 - average) * weight_new
    return (weight_new, moment_new, average_new)


def on_device(
    token_ids,
    lengths,
    loss_positions,
    loss_targets,
    attention_in,
    attention_in_moment,
    attention_in_average,
    attention_out,
    attention_out_moment,
    attention_out_average,
    feed_in,
    feed_in_moment,
    feed_in_average,
    feed_out,
    feed_out_moment,
    feed_out_average,
    embedding,
    embedding_moment,
    embedding_average,
    unembedding,
    unembedding_moment,
    unembedding_average,
    gains_biases,
    gains_biases_moment,
    gains_biases_average,
):
    devices_all = lax.axis_size(("seq", "fsdp"))
    seq_index = lax.axis_index("seq")
    vocab_index = lax.axis_index(("seq", "fsdp"))
    micro_count = token_ids.shape[0]
    half_rows = token_ids.shape[2]
    layer_count = attention_in.shape[0]
    vocab_here = unembedding.shape[0]
    gain_count = (2 * layer_count + 1) * D
    gain_rows = gains_biases[:gain_count].reshape(2 * layer_count + 1, D)
    bias_rows = gains_biases[gain_count:].reshape(layer_count, H)
    stacks = (attention_in, attention_out, feed_in, feed_out)
    low_stacks = tuple((stack_one.astype(jnp.bfloat16) for stack_one in stacks))
    embed_low = embedding.astype(jnp.bfloat16)
    head_low = unembedding.astype(jnp.bfloat16)
    shard_sums = [tuple((jnp.zeros(stack_one.shape[1:], jnp.float32) for stack_one in stacks))]
    embed_grad = jnp.zeros(embedding.shape, jnp.float32)
    head_grad = jnp.zeros(unembedding.shape, jnp.float32)
    gain_grad = jnp.zeros(gain_rows.shape, jnp.float32)
    bias_grad = jnp.zeros(bias_rows.shape, jnp.float32)
    loss_value = jnp.zeros((), jnp.float32)
    for micro_index in range(micro_count):
        token_row = token_ids[micro_index, 0]
        positions = loss_positions[micro_index, 0]
        targets = loss_targets[micro_index, 0]
        counted = (seq_index * half_rows + positions < lengths[micro_index, 0]).astype(jnp.int32)
        all_tokens, all_targets, all_counted = (
            lax.all_gather(token_row[None], ("seq", "fsdp"), axis=0, tiled=True),
            lax.all_gather(targets[None], ("seq", "fsdp"), axis=0, tiled=True),
            lax.all_gather(counted[None], ("seq", "fsdp"), axis=0, tiled=True),
        )
        looked = jnp.take(embed_low, all_tokens, axis=0)
        arrived = lax.all_to_all(looked, ("seq", "fsdp"), split_axis=0, concat_axis=2, tiled=True)
        residual = arrived[0].astype(jnp.float32)
        fetched = [
            (
                lax.all_gather(low_stacks[0][0], ("seq", "fsdp"), axis=0, tiled=True),
                lax.all_gather(low_stacks[1][0], ("seq", "fsdp"), axis=0, tiled=True),
                lax.all_gather(low_stacks[2][0], ("seq", "fsdp"), axis=0, tiled=True),
                lax.all_gather(low_stacks[3][0], ("seq", "fsdp"), axis=0, tiled=True),
            )
        ]
        layer_index = 0
        residual, kept_values = layer_forward(
            residual,
            fetched[layer_index],
            gain_rows[2 * layer_index],
            gain_rows[2 * layer_index + 1],
            bias_rows[layer_index],
        )
        kept_layers = [kept_values]
        final_in = jnp.take(residual, positions, axis=0)
        final_normed, final_inverse = norm_forward(final_in, gain_rows[2 * layer_count])
        gathered = lax.all_gather(
            final_normed.astype(jnp.bfloat16), ("seq", "fsdp"), axis=0, tiled=True
        )
        logits = cross_right(gathered, head_low)
        vocab_ids = vocab_index * vocab_here + jnp.arange(vocab_here)
        target_hits = all_targets.reshape(-1)[:, None] == vocab_ids[None, :]
        row_peak = jnp.max(logits, axis=1)
        exp_sum = jnp.sum(jnp.exp(logits - row_peak[:, None]), axis=1)
        target_part = jnp.sum(jnp.where(target_hits, logits, 0.0), axis=1)
        logit_sum = jnp.sum(logits, axis=1)
        peak_all, spread_all, target_all, logit_all = merged(
            (row_peak, exp_sum, target_part, logit_sum), ("seq", "fsdp"), combine_stats
        )
        log_total = peak_all + jnp.log(spread_all)
        per_row = (
            log_total
            - (1.0 - smooth) * target_all
            - smooth * logit_all / V
            + z_weight * log_total * log_total
        )
        weights_row = all_counted.reshape(-1).astype(jnp.float32)
        scale_micro = 1.0 / (micro_count * jnp.sum(weights_row))
        loss_value = loss_value + jnp.sum(weights_row * per_row) * scale_micro
        soft_rows = jnp.exp(logits - log_total[:, None])
        grad_logits = (
            (weights_row * scale_micro)[:, None]
            * (
                soft_rows * (1.0 + 2.0 * z_weight * log_total)[:, None]
                - (1.0 - smooth) * target_hits.astype(jnp.float32)
                - smooth / V
            )
        ).astype(jnp.bfloat16)
        head_grad = head_grad + cross_left(grad_logits, gathered)
        grad_final = lax.psum_scatter(
            matmul(grad_logits, head_low), ("seq", "fsdp"), scatter_dimension=0, tiled=True
        )
        grad_rows, gain_grad_final = norm_backward(
            final_in, final_inverse, gain_rows[2 * layer_count], grad_final
        )
        grad_resid = jnp.zeros((half_rows, D), jnp.float32).at[positions].add(grad_rows)
        gain_grad = gain_grad.at[2 * layer_count].add(gain_grad_final)
        layer_grads_all = [None] * layer_count
        for layer_index in reversed(range(layer_count)):
            grad_resid, layer_grads, small_grads = layer_backward(
                grad_resid,
                fetched[layer_index],
                gain_rows[2 * layer_index],
                gain_rows[2 * layer_index + 1],
                kept_layers[layer_index],
            )
            layer_grads_all[layer_index] = layer_grads
            gain_grad = (
                gain_grad.at[2 * layer_index]
                .add(small_grads[0])
                .at[2 * layer_index + 1]
                .add(small_grads[1])
            )
            bias_grad = bias_grad.at[layer_index].add(small_grads[2])
        grad_embed = grad_resid.astype(jnp.bfloat16).reshape(
            half_rows, devices_all, D // devices_all
        )
        moved_grads = lax.all_to_all(
            grad_embed, ("seq", "fsdp"), split_axis=1, concat_axis=0, tiled=True
        )
        embed_grad = embed_grad + jax.ops.segment_sum(
            moved_grads[:, 0].astype(jnp.float32), all_tokens.reshape(-1), num_segments=V
        )
        layer_index = 0
        reduce_layer_grads = layer_grads_all[layer_index]
        reduced = (
            lax.psum_scatter(
                reduce_layer_grads[0], ("seq", "fsdp"), scatter_dimension=0, tiled=True
            ),
            lax.psum_scatter(
                reduce_layer_grads[1], ("seq", "fsdp"), scatter_dimension=0, tiled=True
            ),
            lax.psum_scatter(
                reduce_layer_grads[2], ("seq", "fsdp"), scatter_dimension=0, tiled=True
            ),
            lax.psum_scatter(
                reduce_layer_grads[3], ("seq", "fsdp"), scatter_dimension=0, tiled=True
            ),
        )
        shard_sums[layer_index] = tuple(
            (shard_sums[layer_index][part_index] + reduced[part_index] for part_index in range(4))
        )
    owned_grads = [jnp.stack([shard_sums[0][part_index]]) for part_index in range(4)]
    owned_grads = owned_grads + [embed_grad, head_grad]
    square_sum = jnp.zeros((), jnp.float32)
    for grad_part in owned_grads:
        square_sum = square_sum + jnp.sum(grad_part * grad_part)
    small_grad = jnp.concatenate([gain_grad.reshape(-1), bias_grad.reshape(-1)])
    small_total, square_total = lax.psum((small_grad, square_sum), ("seq", "fsdp"))
    grad_norm = jnp.sqrt(square_total + jnp.sum(small_total * small_total))
    factor = jnp.minimum(1.0, clip_limit / grad_norm)
    first = apply_update(
        attention_in, owned_grads[0], attention_in_moment, attention_in_average, factor, rate_layer
    )
    second = apply_update(
        attention_out,
        owned_grads[1],
        attention_out_moment,
        attention_out_average,
        factor,
        rate_layer,
    )
    third = apply_update(
        feed_in, owned_grads[2], feed_in_moment, feed_in_average, factor, rate_layer
    )
    fourth = apply_update(
        feed_out, owned_grads[3], feed_out_moment, feed_out_average, factor, rate_layer
    )
    fifth = apply_update(
        embedding, embed_grad, embedding_moment, embedding_average, factor, rate_embed
    )
    sixth = apply_update(
        unembedding, head_grad, unembedding_moment, unembedding_average, factor, rate_head
    )
    seventh = apply_update(
        gains_biases, small_total, gains_biases_moment, gains_biases_average, factor, rate_layer
    )
    return (
        loss_value,
        grad_norm,
        first[0],
        first[1],
        first[2],
        second[0],
        second[1],
        second[2],
        third[0],
        third[1],
        third[2],
        fourth[0],
        fourth[1],
        fourth[2],
        fifth[0],
        fifth[1],
        fifth[2],
        sixth[0],
        sixth[1],
        sixth[2],
        seventh[0],
        seventh[1],
        seventh[2],
    )


def solution(mesh):
    return jax.shard_map(
        on_device,
        mesh=mesh,
        in_specs=(
            P(None, "fsdp", "seq"),
            P(None, "fsdp"),
            P(None, "fsdp", "seq"),
            P(None, "fsdp", "seq"),
            P(None, ("seq", "fsdp"), None),
            P(None, ("seq", "fsdp"), None),
            P(None, ("seq", "fsdp"), None),
            P(None, ("seq", "fsdp"), None),
            P(None, ("seq", "fsdp"), None),
            P(None, ("seq", "fsdp"), None),
            P(None, ("seq", "fsdp"), None),
            P(None, ("seq", "fsdp"), None),
            P(None, ("seq", "fsdp"), None),
            P(None, ("seq", "fsdp"), None),
            P(None, ("seq", "fsdp"), None),
            P(None, ("seq", "fsdp"), None),
            P(None, ("seq", "fsdp")),
            P(None, ("seq", "fsdp")),
            P(None, ("seq", "fsdp")),
            P(("seq", "fsdp"), None),
            P(("seq", "fsdp"), None),
            P(("seq", "fsdp"), None),
            P(),
            P(),
            P(),
        ),
        out_specs=(
            P(),
            P(),
            P(None, ("seq", "fsdp"), None),
            P(None, ("seq", "fsdp"), None),
            P(None, ("seq", "fsdp"), None),
            P(None, ("seq", "fsdp"), None),
            P(None, ("seq", "fsdp"), None),
            P(None, ("seq", "fsdp"), None),
            P(None, ("seq", "fsdp"), None),
            P(None, ("seq", "fsdp"), None),
            P(None, ("seq", "fsdp"), None),
            P(None, ("seq", "fsdp"), None),
            P(None, ("seq", "fsdp"), None),
            P(None, ("seq", "fsdp"), None),
            P(None, ("seq", "fsdp")),
            P(None, ("seq", "fsdp")),
            P(None, ("seq", "fsdp")),
            P(("seq", "fsdp"), None),
            P(("seq", "fsdp"), None),
            P(("seq", "fsdp"), None),
            P(),
            P(),
            P(),
        ),
        check_vma=False,
    )
```

profile of v0, /device:TPU:0, one launch (start us, length us, event | category | flops | bytes accessed | tf_op | source)
XLA Modules:
  0.0 2407.2 jit_solution(15392797509487333377)
XLA Ops:
  12.9 70.7 %all-gather.1 = s32[32,1,512]{2,1,0:T(1,128)S(1)} all-gather(s32[1,1,512]{2,1,0:T(1,128)S(1)} %get-tuple-element.1349), channel_id=3, replica_groups=mesh['seq'=2,'fsdp'=16] {'seq','fsdp'}, dimensions={0}, use_global_device_ids=true | all-gather | bytes 67584 | tf_op jit(solution)/shard_map/all_gather | solution.py:345
  83.6 7.7 copy.358
  91.4 59.8 %gather_fusion = bf16[16384,24]{1,0:T(8,128)(2,1)} fusion(bf16[32000,24]{1,0:T(8,128)(2,1)} %copy.358, s32[16384]{0:T(1024)S(1)} %broadcast_clamp_fusion.1), kind=kCustom, calls=%fused_computation.clone | custom fusion | bytes 1638400 | tf_op jit(solution)/shard_map/jit(_take)/gather | solution.py:349
  159.7 83.6 %all-gather.12 = s32[32,1,512]{2,1,0:T(1,128)S(1)} all-gather(s32[1,1,512]{2,1,0:T(1,128)S(1)} %get-tuple-element.1348), channel_id=14, replica_groups=mesh['seq'=2,'fsdp'=16] {'seq','fsdp'}, dimensions={0}, use_global_device_ids=true | all-gather | bytes 67584 | tf_op jit(solution)/shard_map/all_gather | solution.py:345
  243.4 59.8 %gather_fusion.2 = bf16[16384,24]{1,0:T(8,128)(2,1)} fusion(bf16[32000,24]{1,0:T(8,128)(2,1)} %copy.358, s32[16384]{0:T(1024)S(1)} %broadcast_clamp_fusion), kind=kCustom, calls=%fused_computation.2.clone | custom fusion | bytes 1638400 | tf_op jit(solution)/shard_map/jit(_take)/gather | solution.py:349
  309.2 65.7 %all-gather.8 = s32[32,1,16]{2,1,0:T(1,128)S(1)} all-gather(s32[1,1,16]{2,1,0:T(1,128)S(1)} %get-tuple-element.1365), channel_id=10, replica_groups=mesh['seq'=2,'fsdp'=16] {'seq','fsdp'}, dimensions={0}, use_global_device_ids=true | all-gather | bytes 2112 | tf_op jit(solution)/shard_map/all_gather | solution.py:346
  376.8 63.4 %all-gather.15 = s32[32,1,16]{2,1,0:T(1,128)S(1)} all-gather(s32[1,1,16]{2,1,0:T(1,128)S(1)} %get-tuple-element.1364), channel_id=17, replica_groups=mesh['seq'=2,'fsdp'=16] {'seq','fsdp'}, dimensions={0}, use_global_device_ids=true | all-gather | bytes 2112 | tf_op jit(solution)/shard_map/all_gather | solution.py:346
  448.7 73.7 %all-gather = s32[32,1,16]{2,1,0:T(1,128)S(1)} all-gather(s32[1,1,16]{2,1,0:T(1,128)S(1)} %get-tuple-element.1369), channel_id=2, replica_groups=mesh['seq'=2,'fsdp'=16] {'seq','fsdp'}, dimensions={0}, use_global_device_ids=true | all-gather | bytes 2112 | tf_op jit(solution)/shard_map/all_gather | solution.py:347
  522.4 65.6 %all-gather.11 = s32[32,1,16]{2,1,0:T(1,128)S(1)} all-gather(s32[1,1,16]{2,1,0:T(1,128)S(1)} %get-tuple-element.1368), channel_id=13, replica_groups=mesh['seq'=2,'fsdp'=16] {'seq','fsdp'}, dimensions={0}, use_global_device_ids=true | all-gather | bytes 2112 | tf_op jit(solution)/shard_map/all_gather | solution.py:347
  628.8 6.7 all_to_all.215
  645.6 35.4 %while.112 = (s32[]{:T(128)}, bf16[2,512,6,64]{1,3,2,0:T(8,128)(2,1)S(1)}, f32[2,6,512]{2,1,0:T(8,128)}, s32[2]{0:T(128)}, bf16[1024,6,64]{0,2,1:T(8,128)(2,1)S(...) while((s32[]{:T(128)}, ...), condition=%wide.region_6.8_spmd, body=%wide.region_3.7_spmd.sunk | while | flops 859305472 | bytes 42869416 | solution.py:110
  691.8 7.2 all_to_all.217
  717.2 40.0 %while.114 = (s32[]{:T(128)}, bf16[2,512,6,64]{1,3,2,0:T(8,128)(2,1)}, f32[2,6,512]{2,1,0:T(8,128)}, s32[2]{0:T(128)}, bf16[1024,6,64]{0,2,1:T(8,128)(2,1)}, /*i...) while((s32[]{:T(128)}, ...), condition=%wide.region_23.26_spmd, body=%wide.region_20.25_spmd.sunk | while | flops 859305472 | bytes 49148644 | solution.py:110
  768.0 6.6 fusion.60
  790.5 5.5 fusion.90
  798.1 5.5 fusion.93
  807.1 68.3 %all_gather.78 = bf16[512,768]{1,0:T(8,128)(2,1)S(1)} all-gather(bf16[16,768]{1,0:T(8,128)(2,1)S(1)} %get-tuple-element.1347), channel_id=1, replica_groups=mesh['seq'=2,'fsdp'=16] {'seq','fsdp'}, dimensions={0}, use_global_device_ids=true | all-gather | bytes 811008 | tf_op jit(solution)/shard_map/all_gather | solution.py:371
  875.4 70.7 %all_gather.86 = bf16[512,768]{1,0:T(8,128)(2,1)S(1)} all-gather(bf16[16,768]{1,0:T(8,128)(2,1)S(1)} %get-tuple-element.1346), channel_id=1, replica_groups=mesh['seq'=2,'fsdp'=16] {'seq','fsdp'}, dimensions={0}, use_global_device_ids=true | all-gather | bytes 811008 | tf_op jit(solution)/shard_map/all_gather | solution.py:371
  951.8 63.7 %all-gather.19 = bf16[32,1,512]{2,1,0:T(2,128)(2,1)S(1)} all-gather(bf16[1,1,512]{2,1,0:T(2,128)(2,1)S(1)} %reshape.1137), channel_id=9, replica_groups=mesh['seq'=2,'fsdp'=16] {'seq','fsdp'}, dimensions={0}, use_global_device_ids=true | all-gather | bytes 33792 | tf_op jit(solution)/shard_map/all_gather | solution.py:28
  1015.5 65.9 %all-gather.20 = bf16[32,1,512]{2,1,0:T(2,128)(2,1)S(1)} all-gather(bf16[1,1,512]{2,1,0:T(2,128)(2,1)S(1)} %reshape.1139), channel_id=11, replica_groups=mesh['seq'=2,'fsdp'=16] {'seq','fsdp'}, dimensions={0}, use_global_device_ids=true | all-gather | bytes 33792 | tf_op jit(solution)/shard_map/all_gather | solution.py:28
  1081.4 63.8 %all-gather.21 = bf16[32,1,512]{2,1,0:T(2,128)(2,1)S(1)} all-gather(bf16[1,1,512]{2,1,0:T(2,128)(2,1)S(1)} %reshape.1141), channel_id=12, replica_groups=mesh['seq'=2,'fsdp'=16] {'seq','fsdp'}, dimensions={0}, use_global_device_ids=true | all-gather | bytes 33792 | tf_op jit(solution)/shard_map/all_gather | solution.py:28
  1145.8 66.1 %all-gather.18 = bf16[32,1,512]{2,1,0:T(2,128)(2,1)S(1)} all-gather(bf16[1,1,512]{2,1,0:T(2,128)(2,1)S(1)} %reshape.1135), channel_id=8, replica_groups=mesh['seq'=2,'fsdp'=16] {'seq','fsdp'}, dimensions={0}, use_global_device_ids=true | all-gather | bytes 33792 | tf_op jit(solution)/shard_map/all_gather | solution.py:28
  1212.5 63.7 %all-gather.23 = bf16[32,1,512]{2,1,0:T(2,128)(2,1)S(1)} all-gather(bf16[1,1,512]{2,1,0:T(2,128)(2,1)S(1)} %reshape.1145), channel_id=16, replica_groups=mesh['seq'=2,'fsdp'=16] {'seq','fsdp'}, dimensions={0}, use_global_device_ids=true | all-gather | bytes 33792 | tf_op jit(solution)/shard_map/all_gather | solution.py:28
  1276.3 66.1 %all-gather.24 = bf16[32,1,512]{2,1,0:T(2,128)(2,1)S(1)} all-gather(bf16[1,1,512]{2,1,0:T(2,128)(2,1)S(1)} %reshape.1147), channel_id=18, replica_groups=mesh['seq'=2,'fsdp'=16] {'seq','fsdp'}, dimensions={0}, use_global_device_ids=true | all-gather | bytes 33792 | tf_op jit(solution)/shard_map/all_gather | solution.py:28
  1342.5 63.7 %all-gather.25 = bf16[32,1,512]{2,1,0:T(2,128)(2,1)S(1)} all-gather(bf16[1,1,512]{2,1,0:T(2,128)(2,1)S(1)} %reshape.1149), channel_id=19, replica_groups=mesh['seq'=2,'fsdp'=16] {'seq','fsdp'}, dimensions={0}, use_global_device_ids=true | all-gather | bytes 33792 | tf_op jit(solution)/shard_map/all_gather | solution.py:28
  1406.2 66.1 %all-gather.22 = bf16[32,1,512]{2,1,0:T(2,128)(2,1)S(1)} all-gather(bf16[1,1,512]{2,1,0:T(2,128)(2,1)S(1)} %reshape.1143), channel_id=15, replica_groups=mesh['seq'=2,'fsdp'=16] {'seq','fsdp'}, dimensions={0}, use_global_device_ids=true | all-gather | bytes 33792 | tf_op jit(solution)/shard_map/all_gather | solution.py:28
  1472.4 45.8 %while.113 = (s32[]{:T(128)}, f32[512]{0:T(512)S(1)}, f32[512]{0:T(512)S(1)}, f32[512]{0:T(512)S(1)}, f32[512]{0:T(512)S(1)}, /*index=5*/bf16[32,512]{1,0:T(8,12...) while((s32[]{:T(128)}, f32[512]{0:T(512)S(1)}, ...), condition=%wide.region_14.17_spmd, body=%wide.region_13.16_spmd.sunk | while | flops 6149 | bytes 37031 | solution.py:40
  1533.7 84.0 %reduce-scatter.9.cloned.1.call-done = f32[16,768]{1,0:T(8,128)} async-done(((f32[512,768]{1,0:T(8,128)}), f32[16,768]{1,0:T(8,128)}) %reduce-scatter.9.cloned.1.call-update) | async-done | bytes 49168 | tf_op jit(solution)/shard_map/reduce_scatter | solution.py:404
  1617.7 102.6 %reduce-scatter.11.cloned.1.call-done = f32[16,768]{1,0:T(8,128)} async-done(((f32[512,768]{1,0:T(8,128)}), f32[16,768]{1,0:T(8,128)}) %reduce-scatter.11.cloned.1.call-update) | async-done | bytes 49168 | tf_op jit(solution)/shard_map/reduce_scatter | solution.py:404
  1724.1 9.6 multiply_convert_fusion.3
  1735.9 7.6 multiply_convert_fusion.5
  1743.5 7.8 fusion.56
  1751.4 7.4 multiply_reduce_fusion.4
  1777.4 70.0 %while.116 = (s32[]{:T(128)}, f32[1024,6,64]{0,2,1:T(8,128)}, f32[1024,6,64]{0,2,1:T(8,128)}, f32[6,1024]{1,0:T(8,128)S(1)}, bf16[2,512,6,64]{1,3,2,0:T(8,128)(2...) while((s32[]{:T(128)}, f32[1024,6,64]{0,2,1:T(8,128)}, ...), condition=%wide.region_42.45_spmd.clone, body=%wide.region_38.44_spmd.clone.sunk | while | flops 2059993600 | bytes 254755888 | solution.py:155
  1785.0 6.5 multiply_reduce_fusion.29
  1791.4 5.5 convert_reduce_fusion.12
  1797.8 5.6 bitcast_add_fusion.20
  1819.6 6.4 multiply_reduce_fusion.29
  1826.1 5.5 convert_reduce_fusion.12
  1832.5 6.0 bitcast_add_fusion.20
  1861.5 6.3 all_to_all.219
  1873.9 7.4 reduce-window.34
  1904.9 70.8 %while.117 = (s32[]{:T(128)}, f32[1024,6,64]{0,2,1:T(8,128)}, f32[1024,6,64]{0,2,1:T(8,128)}, f32[6,1024]{1,0:T(8,128)S(1)}, bf16[2,512,6,64]{1,3,2,0:T(8,128)(2...) while((s32[]{:T(128)}, f32[1024,6,64]{0,2,1:T(8,128)}, ...), condition=%wide.region_54.57_spmd.clone, body=%wide.region_50.56_spmd.clone.sunk | while | flops 2059993600 | bytes 254755888 | solution.py:155
  1912.7 6.5 multiply_reduce_fusion.30
  1919.2 5.5 convert_reduce_fusion.13
  1925.9 5.7 bitcast_add_fusion.22
  1948.0 6.4 multiply_reduce_fusion.30
  1954.4 5.5 convert_reduce_fusion.13
  1960.8 5.9 bitcast_add_fusion.22
  1989.7 6.3 all_to_all.222
  2002.2 7.4 reduce-window.36
  2020.3 5.5 convolution_add_fusion.1
  2026.5 6.4 fusion.78
  2032.9 11.0 convolution_add_fusion
  2043.9 5.4 fusion.64
  2064.3 16.5 all-to-all-done.15
  2084.3 6.2 multiply_reduce_fusion.2
  2097.5 95.1 %scatter_custom_fusion.3 = f32[32000,24]{1,0:T(8,128)} fusion(s32[16384]{0:T(1024)} %bitcast.585, f32[16384,24]{1,0:T(8,128)} %bitcast.567, f32[]{:T(128)} %constant.475.clone.1), kind=kCustom, calls=%fused_computation.108 | custom fusion | flops 393216 | bytes 3072512 | tf_op jit(solution)/shard_map/scatter-add | solution.py:435
  2192.6 10.5 copy.412
  2205.7 6.3 copy.416
  2211.9 94.3 %scatter_custom_fusion.2 = f32[32000,24]{1,0:T(8,128)} fusion(s32[16384]{0:T(1024)} %bitcast.584, f32[16384,24]{1,0:T(8,128)} %bitcast.566, f32[]{:T(128)} %constant.475.clone.1), kind=kCustom, calls=%fused_computation.110 | custom fusion | flops 393216 | bytes 3072512 | tf_op jit(solution)/shard_map/scatter-add | solution.py:435
  2306.2 10.9 copy.411
  2332.4 40.7 %all-reduce.2 = (f32[]{:T(128)}, f32[2316]{0:T(1024)S(1)}) all-reduce(f32[]{:T(128)S(6)} %add.774, f32[2316]{0:T(1024)S(1)} %pad_maximum_fusion.14), channel_id=1, replica_groups=mesh['seq'=2,'fsdp'=16] {'seq','fsdp'}, use_global_device_ids=true, to_apply=%region_74.77 | all-reduce | flops 2317 | bytes 18536 | tf_op jit(solution)/shard_map/psum | solution.py:463
  2375.7 10.1 multiply_add_fusion.2
  (1065 shorter events, 489.1 us)
Async XLA Ops:
  7.2 600.4 %all-gather.31.cloned.1.call-start = ((), (), s32[]{:S(2)}) async-start(), calls=%async_computation.24 | async-start | bytes 3852288 | tf_op jit(solution)/shard_map/all_gather | solution.py:354
  8.9 753.0 %all-gather.33.cloned.1.call-start = ((), (), s32[]{:S(2)}) async-start(), calls=%async_computation.25 | async-start | bytes 1216512 | tf_op jit(solution)/shard_map/all_gather | solution.py:355
  10.4 757.5 %all-gather.35.cloned.1.call-start = ((), (), s32[]{:S(2)}) async-start(), calls=%async_computation.26 | async-start | bytes 6488064 | tf_op jit(solution)/shard_map/all_gather | solution.py:356
  83.6 71.0 %copy-start.91 = (s32[32,1,512]{2,1,0:T(1,128)}, s32[32,1,512]{2,1,0:T(1,128)S(1)}, u32[]{:S(2)}) copy-start(s32[32,1,512]{2,1,0:T(1,128)S(1)} %all-gather.1) | copy-start | bytes 196612
  155.6 288.6 %all-to-all-start = ((bf16[32,512,24]{1,2,0:T(8,128)(2,1)}), bf16[32,512,24]{1,2,0:T(8,128)(2,1)}, u32[]{:S(2)}, u32[]{:S(2)}) async-start(bf16[32,512,24]{1,2,0:T(8,128)(2,1)} %broadcast_select_fusion.1), calls=%async_computation | async-start | bytes 1572864 | tf_op jit(solution)/shard_map/all_to_all | solution.py:350
  159.0 631.5 %all-gather.37.cloned.1.call-start = ((), (), s32[]{:S(2)}) async-start(), calls=%async_computation.27 | async-start | bytes 3244032 | tf_op jit(solution)/shard_map/all_gather | solution.py:357
  243.4 198.8 %copy-start.92 = (s32[32,1,512]{2,1,0:T(1,128)}, s32[32,1,512]{2,1,0:T(1,128)S(1)}, u32[]{:S(2)}) copy-start(s32[32,1,512]{2,1,0:T(1,128)S(1)} %all-gather.12) | copy-start | bytes 196612
  307.9 133.7 %copy-start.151 = (s32[2,1]{0,1:T(1,128)S(1)}, s32[2,1]{0,1:T(1,128)}, u32[]{:S(2)}) copy-start(s32[2,1]{0,1:T(1,128)} %param.58) | copy-start | bytes 28
  309.2 138.2 %copy-start.131 = (s32[2,1,16]{2,1,0:T(1,128)S(1)}, s32[2,1,16]{2,1,0:T(1,128)}, u32[]{:S(2)}) copy-start(s32[2,1,16]{2,1,0:T(1,128)} %param.59) | copy-start | bytes 388
  444.3 157.5 %all-to-all-start.4 = ((bf16[32,512,24]{1,2,0:T(8,128)(2,1)}), bf16[32,512,24]{1,2,0:T(8,128)(2,1)S(1)}, u32[]{:S(2)}, u32[]{:S(2)}) async-start(bf16[32,512,24]{1,2,0:T(8,128)(2,1)} %broadcast_select_fusion), calls=%async_computation.4 | async-start | bytes 1572864 | tf_op jit(solution)/shard_map/all_to_all | solution.py:350
  594.8 18.7 copy-start.89
  616.9 9.9 copy-start.55
  681.0 10.7 copy-start.27
  681.0 10.7 copy-start.28
  681.0 10.7 copy-start.52
  681.0 10.7 copy-start.61
  699.0 58.2 %all-to-all-start.3 = ((bf16[2,512,384]{1,2,0:T(8,128)(2,1)}), bf16[2,512,384]{1,2,0:T(8,128)(2,1)}, u32[]{:S(2)}, u32[]{:S(2)}) async-start(bf16[2,512,384]{1,2,0:T(8,128)(2,1)} %bitcast.572), calls=%async_computation.3 | async-start | bytes 1572864 | tf_op jit(solution)/shard_map/all_to_all | solution.py:180
  717.2 44.6 %copy-start.35 = (f32[512,768]{1,0:T(8,128)S(1)}, f32[512,768]{1,0:T(8,128)}, u32[]{:S(2)}) copy-start(f32[512,768]{1,0:T(8,128)} %copy-done.34) | copy-start | bytes 4718596
  757.2 8.3 all-to-all-start.7
  761.5 856.1 %reduce-scatter.9.cloned.1.call-start = ((), (), s32[]{:S(2)}) async-start(), calls=%async_computation.22 | async-start | bytes 1622016 | tf_op jit(solution)/shard_map/reduce_scatter | solution.py:404
  765.5 993.3 %copy-start.93 = (f32[512]{0:T(512)}, f32[512]{0:T(512)S(1)}, u32[]{:S(2)}) copy-start(f32[512]{0:T(512)S(1)} %get-tuple-element.1359) | copy-start | bytes 6148
  767.9 990.9 %copy-start.31 = (f32[512,768]{1,0:T(8,128)}, f32[512,768]{1,0:T(8,128)S(1)}, u32[]{:S(2)}) copy-start(f32[512,768]{1,0:T(8,128)S(1)} %get-tuple-element.1379) | copy-start | bytes 4718596
  768.0 990.9 %copy-start.100 = (f32[512]{0:T(512)}, f32[512]{0:T(512)S(1)}, u32[]{:S(2)}) copy-start(f32[512]{0:T(512)S(1)} %get-tuple-element.1355) | copy-start | bytes 6148
  806.5 142.3 %copy-start.147 = (f32[16]{0:T(128)}, f32[16]{0:T(128)S(1)}, u32[]{:S(2)}) copy-start(f32[16]{0:T(128)S(1)} %get-tuple-element.1371) | copy-start | bytes 196
  807.0 141.8 %copy-start.145 = (f32[16]{0:T(128)}, f32[16]{0:T(128)S(1)}, u32[]{:S(2)}) copy-start(f32[16]{0:T(128)S(1)} %get-tuple-element.1373) | copy-start | bytes 196
  875.4 70.7 %copy-start.87 = (bf16[512,768]{1,0:T(8,128)(2,1)}, bf16[512,768]{1,0:T(8,128)(2,1)S(1)}, u32[]{:S(2)}) copy-start(bf16[512,768]{1,0:T(8,128)(2,1)S(1)} %all_gather.78) | copy-start | bytes 2359300
  949.9 262.0 %copy-start.76 = (f32[512,1000]{0,1:T(8,128)}, f32[512,1000]{0,1:T(8,128)S(1)}, u32[]{:S(2)}) copy-start(f32[512,1000]{0,1:T(8,128)S(1)} %get-tuple-element.1385) | copy-start | bytes 6144004
  950.2 568.0 %copy-start.138 = (f32[512]{0:T(512)S(1)}, f32[512]{0:T(512)}, u32[]{:S(2)}) copy-start(f32[512]{0:T(512)} %convert_element_type.515) | copy-start | bytes 6148
  1523.4 196.8 %reduce-scatter.11.cloned.1.call-start = ((), (), s32[]{:S(2)}) async-start(), calls=%async_computation.23 | async-start | bytes 1622016 | tf_op jit(solution)/shard_map/reduce_scatter | solution.py:404
  1527.6 192.7 %copy-start.146 = (f32[16]{0:T(128)S(1)}, f32[16]{0:T(128)}, u32[]{:S(2)}) copy-start(f32[16]{0:T(128)} %copy-done.145) | copy-start | bytes 196
  1527.6 192.7 %copy-start.148 = (f32[16]{0:T(128)S(1)}, f32[16]{0:T(128)}, u32[]{:S(2)}) copy-start(f32[16]{0:T(128)} %copy-done.147) | copy-start | bytes 196
  1527.6 194.2 %copy-start.162 = (f32[16]{0:T(128)S(1)}, f32[16]{0:T(128)}, u32[]{:S(2)}) copy-start(f32[16]{0:T(128)} %get-tuple-element.1370) | copy-start | bytes 196
  1532.2 789.8 %reduce-scatter.13.cloned.1.call-start = ((), (), s32[]{:S(2)}) async-start(), calls=%async_computation.28 | async-start | bytes 2433024 | tf_op jit(solution)/shard_map/reduce_scatter | solution.py:444
  1724.1 9.7 copy-start.99
  1724.1 9.7 copy-start.161
  1775.6 548.0 %reduce-scatter.17.cloned.1.call-start = ((), (), s32[]{:S(2)}) async-start(), calls=%async_computation.30 | async-start | bytes 6488064 | tf_op jit(solution)/shard_map/reduce_scatter | solution.py:450
  1797.8 10.4 copy-start.3
  1832.5 10.8 copy-start.3
  1869.5 12.3 copy-start.109
  1869.5 18.9 copy-start.41
  1869.5 18.9 copy-start.58
  1903.3 421.8 %reduce-scatter.19.cloned.1.call-start = ((), (), s32[]{:S(2)}) async-start(), calls=%async_computation.31 | async-start | bytes 7704576
  1925.9 10.6 copy-start.5
  1960.8 10.9 copy-start.5
  1997.7 12.3 copy-start.108
  1997.7 18.2 copy-start.36
  1997.7 18.3 copy-start.90
  1997.7 18.3 copy-start.116
  1997.8 18.3 copy-start.118
  2025.9 302.2 %reduce-scatter.15.cloned.1.call-start = ((), (), s32[]{:S(2)}) async-start(), calls=%async_computation.29 | async-start | bytes 12976128 | tf_op jit(solution)/shard_map/reduce_scatter | solution.py:447
  2054.7 26.1 %all-to-all-start.15 = ((bf16[512,32,24]{0,2,1:T(8,128)(2,1)}), bf16[512,32,24]{0,2,1:T(8,128)(2,1)S(1)}, u32[]{:S(2)}, u32[]{:S(2)}) async-start(bf16[512,32,24]{0,2,1:T(8,128)(2,1)} %bitcast.114), calls=%async_computation.17 | async-start | bytes 1572864 | tf_op jit(solution)/shard_map/all_to_all | solution.py:432
  2063.1 21.1 copy-start.86
  2063.1 21.1 copy-start.134
  2063.1 21.1 copy-start.142
  2063.1 21.1 copy-start.157
  2063.1 21.1 copy-start.159
  2080.8 122.3 %all-to-all-start.14 = ((bf16[512,32,24]{0,2,1:T(8,128)(2,1)}), bf16[512,32,24]{0,2,1:T(8,128)(2,1)}, u32[]{:S(2)}, u32[]{:S(2)}) async-start(bf16[512,32,24]{0,2,1:T(8,128)(2,1)} %bitcast.109), calls=%async_computation.16 | async-start | bytes 1572864 | tf_op jit(solution)/shard_map/all_to_all | solution.py:432
  2317.1 57.9 %copy-start.120 = (f32[2316]{0:T(1024)S(1)}, f32[2316]{0:T(1024)}, u32[]{:S(2)}) copy-start(f32[2316]{0:T(1024)} %param.79) | copy-start | bytes 27796
  2317.1 58.0 %copy-start.129 = (f32[2316]{0:T(1024)S(1)}, f32[2316]{0:T(1024)}, u32[]{:S(2)}) copy-start(f32[2316]{0:T(1024)} %param.81) | copy-start | bytes 27796
  2317.1 58.0 %copy-start.130 = (f32[2316]{0:T(1024)S(1)}, f32[2316]{0:T(1024)}, u32[]{:S(2)}) copy-start(f32[2316]{0:T(1024)} %param.80) | copy-start | bytes 27796
  2375.7 10.1 copy-start.49
  2375.7 10.1 copy-start.51
  2375.7 10.1 copy-start.68
  2375.7 11.4 copy-start.69
  (139 other events, 636.0 us)
Sparse Core Ops, SparseCore 0:
  11.4 63.5 all-gather.30
  78.5 52.5 all-gather.32
  134.5 77.8 all-gather.34
  215.7 57.5 all-gather.36
  1523.6 94.0 reduce-scatter.8
  1623.3 96.8 reduce-scatter.10
  1775.7 98.5 reduce-scatter.12
  1903.4 114.0 reduce-scatter.16
  2026.0 132.4 reduce-scatter.18
  2164.3 153.7 reduce-scatter.14
where the time goes:
time: 2420 us; the launch traced here: 2410 us
  blocking collectives  1170 us (48%)
  other arithmetic  394 us (16%)
  local copies, waits for them, and re-layouts  304 us (13%)
  matrix products  264 us (11%)
  waiting for transfers between devices  203 us (8%)
  between operations  27 us (1%)
    all_gather x8, blocking collectives, merged(): lax.all_gather(a.astype(kind), axis)  519 us
    scatter-add x2, other arithmetic, on_device(): jax.ops.segment_sum(moved_grads[:, 0].astype(jnp.float32), all_tokens.res...  189 us
    reduce_scatter x2, waiting for transfers between devices, on_device(): lax.psum_scatter(matmul(grad_logits, head_low), ('seq', 'fsdp'), scatter_...  187 us
    all_gather x2, blocking collectives, on_device(): lax.all_gather(token_row[None], ('seq', 'fsdp'), axis=0, tiled=True)  154 us
    all_gather x2, blocking collectives, on_device(): lax.all_gather(counted[None], ('seq', 'fsdp'), axis=0, tiled=True)  139 us
    all_gather x2, blocking collectives, on_device(): lax.all_gather(final_normed.astype(jnp.bfloat16), ('seq', 'fsdp'), axis=0...  139 us
    all_gather x2, blocking collectives, on_device(): lax.all_gather(targets[None], ('seq', 'fsdp'), axis=0, tiled=True)  129 us
    gather x4, local copies, waits for them, and re-layouts, on_device(): looked = jnp.take(embed_low, all_tokens, axis=0)  128 us
  transfers between devices with their start and end apart: 16, of which 3 were waited for; matrix products, arithmetic and copies ran while one was open for 33% of the time, Pallas kernels for 0%

commit v1 on v0

v1 whole, which is shorter than its diff:
```python
import functools

import jax
import jax.numpy as jnp
from jax import lax
from jax.experimental import pallas as pl
from jax.experimental.pallas import tpu as pltpu
from jax.sharding import PartitionSpec as P

D = 768
H = 12
HD = 64
FF = 2048
V = 32000


epsilon = 1e-06
smooth = 0.1
z_weight = 0.005
clip_limit = 0.5
moment = 0.9
average = 0.9
rate_layer = 200.0
rate_head = 1000.0
rate_embed = 5000.0
negative = -1e30
both = ("seq", "fsdp")
highest = lax.Precision.HIGHEST
MESH = pl.DeviceIdType.MESH


def dot(left_side, right_side, left_axis, right_axis, precision=None):
    return lax.dot_general(
        left_side,
        right_side,
        (((left_axis,), (right_axis,)), ((), ())),
        precision=precision,
        preferred_element_type=jnp.float32,
    )


def line_of(fsdp_count):
    return 4 if fsdp_count % 4 == 0 else 1


def gather_kernel(cores, fsdp, x_ref, o_ref, send_sem, recv_sem):
    plane = line_of(fsdp)
    lines = fsdp // plane
    core = lax.axis_index("seq")
    spot = lax.axis_index("fsdp")
    high, low = spot // plane, spot % plane
    line_peers = [((high + k) % lines) * plane + low for k in range(1, lines)]
    plane_peers = [high * plane + (low + k) % plane for k in range(1, plane)]
    core_peers = [(core + k) % cores for k in range(1, cores)]
    peers = [(core, p) for p in line_peers + plane_peers] + [(c, spot) for c in core_peers]

    barrier = pltpu.get_barrier_semaphore()
    for peer in peers:
        pl.semaphore_signal(barrier, inc=1, device_id=peer, device_id_type=MESH)
    pl.semaphore_wait(barrier, len(peers))

    sent = []

    def send(source_ref, block, peer):
        copy = pltpu.make_async_remote_copy(
            src_ref=source_ref,
            dst_ref=o_ref.at[block],
            send_sem=send_sem.at[len(sent)],
            recv_sem=recv_sem.at[block],
            device_id=peer,
            device_id_type=MESH,
        )
        copy.start()
        sent.append(copy)

    def arrived(block):
        pltpu.make_async_copy(o_ref.at[block], o_ref.at[block], recv_sem.at[block]).wait()

    mine = core * fsdp + spot
    for p in line_peers:
        send(x_ref, mine, (core, p))
    for p in plane_peers:
        send(x_ref, mine, (core, p))
    for c in core_peers:
        send(x_ref, mine, (c, spot))
    o_ref[mine] = x_ref[...]
    for k in range(1, lines):
        block = core * fsdp + ((high + lines - k) % lines) * plane + low
        arrived(block)
        for p in plane_peers:
            send(o_ref.at[block], block, (core, p))
        for c in core_peers:
            send(o_ref.at[block], block, (c, spot))
    for m in range(lines):
        for k in range(1, plane):
            block = core * fsdp + ((high + lines - m) % lines) * plane + (low + plane - k) % plane
            arrived(block)
            for c in core_peers:
                send(o_ref.at[block], block, (c, spot))
    for c in core_peers:
        for m in range(lines):
            for k in range(plane):
                block = c * fsdp + ((high + lines - m) % lines) * plane + (low + plane - k) % plane
                arrived(block)
    for copy in sent:
        copy.wait_send()


def gather_rows(array, collective):
    cores, fsdp = lax.axis_size("seq"), lax.axis_size("fsdp")
    count = cores * fsdp
    return pl.pallas_call(
        functools.partial(gather_kernel, cores, fsdp),
        out_shape=jax.ShapeDtypeStruct((count,) + array.shape, array.dtype),
        in_specs=[pl.BlockSpec(memory_space=pltpu.VMEM)],
        out_specs=pl.BlockSpec(memory_space=pltpu.VMEM),
        scratch_shapes=[
            pltpu.SemaphoreType.DMA((count,)),
            pltpu.SemaphoreType.DMA((count,)),
        ],
        compiler_params=pltpu.CompilerParams(collective_id=collective, has_side_effects=True),
        name="gather_rows",
    )(array)


def other_core(arrays):
    return lax.ppermute(arrays, "seq", [(0, 1), (1, 0)])


def norm_forward(values, gain_row):
    inverse = lax.rsqrt(jnp.mean(values * values, axis=-1, keepdims=True) + epsilon)
    return (values * inverse * gain_row, inverse)


def norm_backward(values, inverse, gain_row, grad_out):
    scaled = grad_out * gain_row
    grad_gain = jnp.sum(grad_out * values * inverse, axis=0)
    grad_in = inverse * scaled - values * inverse**3 * jnp.mean(
        values * scaled, axis=-1, keepdims=True
    )
    return (grad_in, grad_gain)


def apply_update(weight_old, grad_full, moment_old, average_old, factor, rate):
    clipped = factor * grad_full
    moment_new = moment * moment_old + clipped
    weight_new = weight_old - rate * (clipped + moment * moment_new)
    average_new = average * average_old + (1.0 - average) * weight_new
    return (weight_new, moment_new, average_new)


def on_device(
    token_ids,
    lengths,
    loss_positions,
    loss_targets,
    attention_in,
    attention_in_moment,
    attention_in_average,
    attention_out,
    attention_out_moment,
    attention_out_average,
    feed_in,
    feed_in_moment,
    feed_in_average,
    feed_out,
    feed_out_moment,
    feed_out_average,
    embedding,
    embedding_moment,
    embedding_average,
    unembedding,
    unembedding_moment,
    unembedding_average,
    gains_biases,
    gains_biases_moment,
    gains_biases_average,
):
    low = jnp.bfloat16
    wide = jnp.float32
    devices_all = lax.axis_size(both)
    seq_index = lax.axis_index("seq")
    device = lax.axis_index(both)
    micros, _, half = token_ids.shape
    loss_dev = loss_positions.shape[2]
    tokens = micros * half
    rows = micros * loss_dev
    rows_all = devices_all * rows
    vocab_here = unembedding.shape[0]
    features = D // devices_all
    gate_here = FF // devices_all
    gain_rows = gains_biases[: 3 * D].reshape(3, D)
    bias_row = gains_biases[3 * D :]
    second = seq_index.astype(wide)

    positions = loss_positions[:, 0]
    targets = loss_targets[:, 0]
    counted = (seq_index * half + positions < lengths[:, :1]).astype(jnp.int32)
    labels = jnp.concatenate([targets.reshape(-1), counted.reshape(-1)])
    ids_block = jnp.concatenate([token_ids.reshape(-1), labels])
    pad = -ids_block.shape[0] % 1024
    ids_block = jnp.pad(ids_block, (0, pad)).reshape(-1, 128)
    ids_all = gather_rows(ids_block, 1).reshape(devices_all, -1)
    all_tokens = ids_all[:, :tokens]
    all_targets = ids_all[:, tokens : tokens + rows].reshape(-1)
    all_counted = ids_all[:, tokens + rows : tokens + 2 * rows]

    w_in = lax.all_gather(attention_in[0].astype(low), both, axis=0, tiled=True)
    w_out = lax.all_gather(attention_out[0].astype(low), both, axis=0, tiled=True)
    w_feed = lax.all_gather(feed_in[0].astype(low), both, axis=0, tiled=True)
    w_down = lax.all_gather(feed_out[0].astype(low), both, axis=0, tiled=True)
    head_low = unembedding.astype(low)

    looked = jnp.take(embedding.astype(low), all_tokens, axis=0)
    arrived = lax.all_to_all(
        jnp.swapaxes(looked, 1, 2), both, split_axis=0, concat_axis=0, tiled=True
    )
    x_t = arrived.reshape(D, tokens)
    x_wide = x_t.astype(wide)
    inverse_one = lax.rsqrt(jnp.mean(x_wide * x_wide, axis=0, keepdims=True) + epsilon)
    normed_t = (x_wide * inverse_one * gain_rows[0][:, None]).astype(low)

    project_t = dot(w_in[:, D:], normed_t, 0, 0)
    kv_t = project_t[: 2 * D].astype(low)
    forget_t = (project_t[2 * D :] + bias_row[:, None]).astype(low).astype(wide)
    pick = [
        (positions[m][:, None] == jnp.arange(half)[None, :]).astype(low) for m in range(micros)
    ]

    def per_micro(array, m):
        return array[:, m * half : (m + 1) * half]

    x_rows = jnp.concatenate([dot(pick[m], per_micro(x_t, m), 1, 1) for m in range(micros)])
    normed_rows = jnp.concatenate(
        [dot(pick[m], per_micro(normed_t, m), 1, 1) for m in range(micros)]
    ).astype(low)
    q_rows = dot(normed_rows, w_in[:, :D], 1, 0).astype(low)

    upper = (jnp.arange(half)[:, None] <= jnp.arange(half)[None, :]).astype(wide)
    log_gate = jax.nn.log_sigmoid(forget_t).reshape(H, micros, half)
    decay_own = lax.dot_general(
        log_gate, upper, (((2,), (0,)), ((), ())), precision=highest, preferred_element_type=wide
    )
    total_own = decay_own[:, :, -1]
    decay_rows = jnp.stack(
        [dot(pick[m].astype(wide), decay_own[:, m], 1, 1, highest) for m in range(micros)]
    )
    q_own = q_rows.reshape(micros, loss_dev, H, HD)
    q_far, decay_far, total_far, place_far = other_core((q_own, decay_rows, total_own, positions))
    shift_own = second * total_far
    shift_far = (1.0 - second) * total_own
    key_decay = decay_own + shift_own[:, :, None]
    row_decay = jnp.concatenate(
        [decay_rows + shift_own.T[:, None], decay_far + shift_far.T[:, None]], axis=1
    )
    q_all = jnp.concatenate([q_own, q_far], axis=1)
    places = jnp.concatenate(
        [positions + seq_index * half, place_far + (1 - seq_index) * half], axis=1
    )
    key_places = seq_index * half + jnp.arange(half)
    keys_t = kv_t[:D].reshape(H, HD, tokens)
    values_t = kv_t[D:].reshape(H, HD, tokens)

    scores = []
    for m in range(micros):
        keys_m = keys_t[:, :, m * half : (m + 1) * half]
        raw = jnp.einsum("rhd,hdj->hrj", q_all[m], keys_m, preferred_element_type=wide)
        part = raw * HD ** (-0.5) + row_decay[m].T[:, :, None] - key_decay[:, m][:, None, :]
        causal = places[m][:, None] >= key_places[None, :]
        scores.append(jnp.where(causal[None], part, negative))
    scores = jnp.stack(scores)
    peak_own = jnp.max(scores, axis=-1)
    spread_own = jnp.sum(jnp.exp(scores - peak_own[..., None]), axis=-1)
    peak_far, spread_far = other_core((peak_own, spread_own))

    def swap_rows(array):
        return jnp.concatenate([array[:, :, loss_dev:], array[:, :, :loss_dev]], axis=2)

    peak_far, spread_far = swap_rows(peak_far), swap_rows(spread_far)
    peak = jnp.maximum(peak_own, peak_far)
    log_total = peak + jnp.log(
        spread_own * jnp.exp(peak_own - peak) + spread_far * jnp.exp(peak_far - peak)
    )
    probs = jnp.exp(scores - log_total[..., None])
    probs_low = probs.astype(low)
    probs_rest = (probs - probs_low.astype(wide)).astype(low)

    def mix(weights):
        return jnp.stack(
            [
                jnp.einsum(
                    "hrj,hdj->rhd",
                    weights[m],
                    values_t[:, :, m * half : (m + 1) * half],
                    preferred_element_type=wide,
                )
                for m in range(micros)
            ]
        )

    mixed_part = mix(probs_low)
    rest_part = mix(probs_rest)
    mixed_far, rest_far = other_core((mixed_part[:, loss_dev:], rest_part[:, loss_dev:]))
    mixed_sum = mixed_part[:, :loss_dev] + mixed_far
    mixed_full = mixed_sum + rest_part[:, :loss_dev] + rest_far
    mixed_rows = mixed_sum.reshape(rows, D).astype(low)

    middle = x_rows + dot(mixed_rows, w_out, 1, 0)
    normed_two, inverse_two = norm_forward(middle, gain_rows[1])
    normed_two = normed_two.astype(low)
    gate_up = dot(normed_two, w_feed, 1, 0)
    gate_half, up_half = gate_up[:, :FF], gate_up[:, FF:]
    gate_sigmoid = jax.nn.sigmoid(gate_half)
    hidden = (gate_half * gate_sigmoid * up_half).astype(low)
    final_in = middle + dot(hidden, w_down, 1, 0)
    final_normed, final_inverse = norm_forward(final_in, gain_rows[2])

    final_all = gather_rows(final_normed.astype(low), 2).reshape(rows_all, D)
    logits = dot(final_all, head_low, 1, 1)
    vocab_ids = device * vocab_here + jnp.arange(vocab_here)
    target_hits = all_targets[:, None] == vocab_ids[None, :]
    row_peak = jnp.max(logits, axis=1)
    exp_sum = jnp.sum(jnp.exp(logits - row_peak[:, None]), axis=1)
    target_part = jnp.sum(jnp.where(target_hits, logits, 0.0), axis=1)
    logit_sum = jnp.sum(logits, axis=1)
    stats = jnp.stack([row_peak, exp_sum, target_part, logit_sum])
    stats_all = gather_rows(stats.reshape(-1, 128), 3).reshape(devices_all, 4, rows_all)
    peak_all = jnp.max(stats_all[:, 0], axis=0)
    spread_all = jnp.sum(stats_all[:, 1] * jnp.exp(stats_all[:, 0] - peak_all), axis=0)
    target_all = jnp.sum(stats_all[:, 2], axis=0)
    logit_all = jnp.sum(stats_all[:, 3], axis=0)
    total_all = peak_all + jnp.log(spread_all)
    per_row = (
        total_all
        - (1.0 - smooth) * target_all
        - smooth * logit_all / V
        + z_weight * total_all * total_all
    )
    weights_row = all_counted.astype(wide).reshape(devices_all, micros, loss_dev)
    counts = jnp.sum(weights_row, axis=(0, 2))
    weights_row = (weights_row / (micros * counts)[None, :, None]).reshape(-1)
    loss_value = jnp.sum(weights_row * per_row)
    soft_rows = jnp.exp(logits - total_all[:, None])
    grad_logits = (
        weights_row[:, None]
        * (
            soft_rows * (1.0 + 2.0 * z_weight * total_all)[:, None]
            - (1.0 - smooth) * target_hits.astype(wide)
            - smooth / V
        )
    ).astype(low)
    head_grad = dot(grad_logits, final_all, 0, 0)
    grad_final = lax.psum_scatter(
        dot(grad_logits, head_low, 1, 0), both, scatter_dimension=0, tiled=True
    )

    grad_rows, gain_grad_final = norm_backward(final_in, final_inverse, gain_rows[2], grad_final)
    grad_branch = grad_rows.astype(low)
    grad_hidden = dot(grad_branch, w_down, 1, 1)
    grad_gate = grad_hidden * up_half * gate_sigmoid * (1.0 + gate_half * (1.0 - gate_sigmoid))
    grad_up = grad_hidden * gate_half * gate_sigmoid
    grad_gate_up = jnp.concatenate([grad_gate, grad_up], axis=1).astype(low)
    grad_two, gain_grad_two = norm_backward(
        middle, inverse_two, gain_rows[1], dot(grad_gate_up, w_feed, 1, 1)
    )
    grad_middle = grad_rows + grad_two
    grad_mid_low = grad_middle.astype(low)
    grad_mixed = dot(grad_mid_low, w_out, 1, 1).astype(low)

    normed_two_all = lax.all_gather(normed_two, both, axis=0, tiled=True)
    grad_branch_all = lax.all_gather(grad_branch, both, axis=0, tiled=True)
    hidden_columns = lax.all_to_all(
        hidden.reshape(rows, devices_all, gate_here), both, split_axis=1, concat_axis=0, tiled=True
    ).reshape(rows_all, gate_here)
    grad_down = dot(hidden_columns, grad_branch_all, 0, 0)
    gate_up_columns = lax.all_to_all(
        grad_gate_up.reshape(rows, 2, devices_all, gate_here),
        both,
        split_axis=2,
        concat_axis=0,
        tiled=True,
    ).reshape(rows_all, 2 * gate_here)
    grad_feed_columns = dot(normed_two_all, gate_up_columns, 0, 0)
    grad_feed = lax.all_to_all(
        grad_feed_columns.reshape(devices_all, features, 2 * gate_here),
        both,
        split_axis=0,
        concat_axis=0,
        tiled=True,
    )
    grad_feed = (
        grad_feed.reshape(devices_all, features, 2, gate_here)
        .transpose(1, 2, 0, 3)
        .reshape(features, 2 * FF)
    )
    grad_out = lax.psum_scatter(
        dot(mixed_rows, grad_mid_low, 0, 0), both, scatter_dimension=0, tiled=True
    )

    grad_own = grad_mixed.reshape(micros, loss_dev, H, HD)
    inner_own = jnp.sum(grad_own.astype(wide) * mixed_full, axis=-1)
    grad_far, inner_far = other_core((grad_own, inner_own))
    grad_heads = jnp.concatenate([grad_own, grad_far], axis=1)
    inner_sum = jnp.concatenate([inner_own, inner_far], axis=1)
    query_parts, score_rows = [], []
    grad_keys, grad_values, score_columns = [], [], []
    for m in range(micros):
        keys_m = keys_t[:, :, m * half : (m + 1) * half]
        values_m = values_t[:, :, m * half : (m + 1) * half]
        grad_probs = jnp.einsum("rhd,hdj->hrj", grad_heads[m], values_m, preferred_element_type=wide)
        grad_scores = (probs[m] * (grad_probs - inner_sum[m].T[:, :, None])).astype(low)
        query_parts.append(
            jnp.einsum("hrj,hdj->rhd", grad_scores, keys_m, preferred_element_type=wide)
        )
        grad_keys.append(
            jnp.einsum("hrj,rhd->hdj", grad_scores, q_all[m], preferred_element_type=wide)
            * HD ** (-0.5)
        )
        grad_values.append(
            jnp.einsum("hrj,rhd->hdj", probs_low[m], grad_heads[m], preferred_element_type=wide)
        )
        score_wide = grad_scores.astype(wide)
        score_rows.append(jnp.sum(score_wide, axis=-1))
        score_columns.append(jnp.sum(score_wide, axis=1))
    query_parts = jnp.stack(query_parts)
    score_rows = jnp.stack(score_rows).transpose(0, 2, 1)
    query_far, score_far = other_core((query_parts[:, loss_dev:], score_rows[:, loss_dev:]))
    grad_query = ((query_parts[:, :loss_dev] + query_far) * HD ** (-0.5)).astype(low)
    grad_query = grad_query.reshape(rows, D)
    rows_sum = score_rows[:, :loss_dev] + score_far
    later = (1.0 - second) * jnp.sum(score_rows[:, loss_dev:], axis=1)
    grad_log = []
    for m in range(micros):
        placed = dot(rows_sum[m], pick[m].astype(wide), 0, 0, highest)
        change = placed - score_columns[m]
        suffix = dot(change, upper, 1, 1, highest)
        grad_log.append(suffix + later[m][:, None])
    grad_log = jnp.concatenate(grad_log, axis=1)
    grad_forget = (grad_log * jax.nn.sigmoid(-forget_t)).astype(low)
    query_t = jnp.concatenate(
        [
            dot(grad_query[m * loss_dev : (m + 1) * loss_dev], pick[m], 0, 0).astype(low)
            for m in range(micros)
        ],
        axis=1,
    )
    keys_part = jnp.concatenate(grad_keys, axis=2).reshape(D, tokens).astype(low)
    values_part = jnp.concatenate(grad_values, axis=2).reshape(D, tokens).astype(low)
    grad_project = jnp.concatenate([query_t, keys_part, values_part, grad_forget], axis=0)
    grad_bias = jnp.sum(grad_forget.astype(wide), axis=1)
    grad_in = lax.psum_scatter(
        dot(normed_t, grad_project, 1, 1), both, scatter_dimension=0, tiled=True
    )
    grad_normed = dot(w_in, grad_project, 1, 0)
    scaled = grad_normed * gain_rows[0][:, None]
    gain_grad_one = jnp.sum(grad_normed * x_wide * inverse_one, axis=1)
    grad_one = inverse_one * scaled - x_wide * inverse_one**3 * jnp.mean(
        x_wide * scaled, axis=0, keepdims=True
    )
    middle_t = jnp.concatenate(
        [
            dot(
                grad_middle[m * loss_dev : (m + 1) * loss_dev],
                pick[m].astype(wide),
                0,
                0,
                highest,
            )
            for m in range(micros)
        ],
        axis=1,
    )
    grad_embed = (middle_t + grad_one).astype(low).reshape(devices_all, features, tokens)
    moved = lax.all_to_all(grad_embed, both, split_axis=0, concat_axis=0, tiled=True)
    embed_grad = jax.ops.segment_sum(
        jnp.swapaxes(moved, 1, 2).reshape(-1, features).astype(wide),
        all_tokens.reshape(-1),
        num_segments=V,
    )

    owned_grads = [grad_in[None], grad_out[None], grad_feed[None], grad_down[None]]
    owned_grads = owned_grads + [embed_grad, head_grad]
    square_sum = jnp.zeros((), wide)
    for grad_part in owned_grads:
        square_sum = square_sum + jnp.sum(grad_part * grad_part)
    small_grad = jnp.concatenate(
        [gain_grad_one, gain_grad_two, gain_grad_final, grad_bias, square_sum[None]]
    )
    small_count = small_grad.shape[0]
    small_grad = jnp.pad(small_grad, (0, -small_count % 1024)).reshape(-1, 128)
    small_sum = jnp.sum(gather_rows(small_grad, 4), axis=0).reshape(-1)
    small_total, square_total = small_sum[: small_count - 1], small_sum[small_count - 1]
    grad_norm = jnp.sqrt(square_total + jnp.sum(small_total * small_total))
    factor = jnp.minimum(1.0, clip_limit / grad_norm)
    updates = (
        (attention_in, owned_grads[0], attention_in_moment, attention_in_average, rate_layer),
        (attention_out, owned_grads[1], attention_out_moment, attention_out_average, rate_layer),
        (feed_in, owned_grads[2], feed_in_moment, feed_in_average, rate_layer),
        (feed_out, owned_grads[3], feed_out_moment, feed_out_average, rate_layer),
        (embedding, embed_grad, embedding_moment, embedding_average, rate_embed),
        (unembedding, head_grad, unembedding_moment, unembedding_average, rate_head),
        (gains_biases, small_total, gains_biases_moment, gains_biases_average, rate_layer),
    )
    results = [loss_value, grad_norm]
    for weight, grad_full, moment_old, average_old, rate in updates:
        results.extend(apply_update(weight, grad_full, moment_old, average_old, factor, rate))
    return tuple(results)


def solution(mesh):
    rows = P(None, both, None)
    tables = (rows,) * 12 + (P(None, both),) * 3 + (P(both, None),) * 3 + (P(),) * 3
    return jax.shard_map(
        on_device,
        mesh=mesh,
        in_specs=(
            P(None, "fsdp", "seq"),
            P(None, "fsdp"),
            P(None, "fsdp", "seq"),
            P(None, "fsdp", "seq"),
        )
        + tables,
        out_specs=(P(), P()) + tables,
        check_vma=False,
    )
```

time: 2420 us -> 939 us (0.39)
  blocking collectives: 1170 us -> 0 us
  matrix products: 264 us -> 92.9 us
  other arithmetic: 394 us -> 261 us
  local copies, waits for them, and re-layouts: 304 us -> 201 us
  waiting for transfers between devices: 203 us -> 278 us
  Pallas kernels: 0 us -> 57.3 us
    all_gather x16 -> x0, blocking collectives: 1080 us -> none  [the longest x8 519 us: merged(): lax.all_gather(a.astype(kind), axis)]
    dot_general x58 -> x45, matrix products: 264 us -> 92.9 us  [the longest x30 80.5 us: dot(): lax.dot_general(left_side, right_side, (((left_axis,), (right_axis,)), ((...]
    pallas_call x0 -> x4, Pallas kernels: none -> 57.3 us  [gather_rows(): pl.pallas_call(functools.partial(gather_kernel, cores, fsdp), out_shape=j...]
    all_to_all x6 -> x5, waiting for transfers between devices: 16.6 us -> 72.1 us  [the longest x1 55.5 us: on_device(): lax.all_to_all(jnp.swapaxes(looked, 1, 2), both, split_axis=0, concat_axi...]
    all_to_all x10 -> x0, blocking collectives: 50.6 us -> none  [the longest x2 13.9 us: layer_forward(): lax.all_to_all(heads_part, 'seq', split_axis=2, concat_axis=0, tiled=True)]
    convert_element_type x148 -> x18, other arithmetic: 65.9 us -> 17.6 us  [the longest x1 2.15 us: on_device(): (middle_t + grad_one).astype(low).reshape(devices_all, features, tokens)]
    psum x1 -> x0, blocking collectives: 40.7 us -> none  [on_device(): lax.psum((small_grad, square_sum), ('seq', 'fsdp'))]
    reduce_sum x15 -> x12, other arithmetic: 46.8 us -> 12.6 us  [the longest x1 3.08 us: on_device(): target_all = jnp.sum(stats_all[:, 2], axis=0)]
  transfers between devices with their start and end apart: 16 -> 26, of which waited for: 3 -> 10; matrix products, arithmetic and copies ran while one was open for 33% -> 53% of each run, Pallas kernels for 0% -> 2%
where the time goes in v1:
time: 939 us; the launch traced here: 933 us
  waiting for transfers between devices  278 us (30%)
  other arithmetic  261 us (28%)
  local copies, waits for them, and re-layouts  201 us (21%)
  matrix products  92.9 us (10%)
  Pallas kernels  57.3 us (6%)
  between operations  21.8 us (2%)
  starting transfers between devices  21.3 us (2%)
    scatter-add x1, other arithmetic, on_device(): jax.ops.segment_sum(jnp.swapaxes(moved, 1, 2).reshape(-1, features).astyp...  181 us
    gather x2, local copies, waits for them, and re-layouts, on_device(): looked = jnp.take(embedding.astype(low), all_tokens, axis=0)  120 us
    reduce_scatter x1, waiting for transfers between devices, on_device(): lax.psum_scatter(dot(grad_logits, head_low, 1, 0), both, scatter_dimensio...  99.5 us
    reduce_scatter x1, waiting for transfers between devices, on_device(): lax.psum_scatter(dot(mixed_rows, grad_mid_low, 0, 0), both, scatter_dimen...  81.7 us
    dot_general x30, matrix products, dot(): lax.dot_general(left_side, right_side, (((left_axis,), (right_axis,)), ((...  80.5 us
    pallas_call x4, Pallas kernels, gather_rows(): pl.pallas_call(functools.partial(gather_kernel, cores, fsdp), out_shape=j...  57.3 us
    all_to_all x1, waiting for transfers between devices, on_device(): lax.all_to_all(jnp.swapaxes(looked, 1, 2), both, split_axis=0, concat_axi...  55.5 us
    all_gather x1, waiting for transfers between devices, on_device(): w_down = lax.all_gather(feed_out[0].astype(low), both, axis=0, tiled=True)  21.9 us
  transfers between devices with their start and end apart: 26, of which 10 were waited for; matrix products, arithmetic and copies ran while one was open for 53% of the time, Pallas kernels for 2%

profile of v1, /device:TPU:0, one launch (start us, length us, event | category | flops | bytes accessed | tf_op | source)
XLA Modules:
  0.0 932.6 jit_solution(16144843361723908082)
XLA Ops:
  7.2 1.6 convert_element_type.166
  10.5 1.7 convert_element_type.178
  12.2 2.0 convert_element_type.162
  14.3 6.0 copy.181
  22.5 14.8 %gather_rows.4 = s32[32,16,128]{2,1,0:T(8,128)} custom-call(s32[16,128]{1,0:T(8,128)} %pad_bitcast_fusion.1.x_ref), custom_call_target="tpu_custom_call" | custom-call | tf_op jit(solution)/shard_map/gather_rows/pallas_call | solution.py:112
  39.2 113.7 %gather_fusion = bf16[32768,24]{1,0:T(8,128)(2,1)} fusion(bf16[32000,24]{1,0:T(8,128)(2,1)} %copy.181, s32[32768]{0:T(1024)S(1)} %broadcast_clamp_fusion), kind=kCustom, calls=%fused_computation | custom fusion | bytes 3276800 | tf_op jit(solution)/shard_map/jit(_take)/gather | solution.py:214
  152.9 6.7 copy.182
  161.1 3.4 all-to-all-start
  168.8 55.5 %all-to-all-done = bf16[32,24,1024]{2,1,0:T(8,128)(2,1)S(1)} async-done(((bf16[32,24,1024]{2,1,0:T(8,128)(2,1)}), bf16[32,24,1024]{2,1,0:T(8,128)(2,1)S(1)}, u32[]{:S(2)}, u32[]{:S(2)}) %all-to-all-start) | async-done | bytes 1572896 | tf_op jit(solution)/shard_map/all_to_all | solution.py:215
  226.3 6.2 fusion.178
  232.6 2.7 copy-done.75
  236.3 3.4 fusion.172
  239.7 2.2 fusion.52
  253.4 1.6 convert_element_type.174
  255.1 1.7 multiply_reduce_fusion.11
  257.5 4.0 fusion.4
  263.0 21.9 %all-gather.21.cloned.1.call-done = bf16[1,2048,768]{2,1,0:T(8,128)(2,1)} async-done(((bf16[1,64,768]{2,1,0:T(8,128)(2,1)}), bf16[1,2048,768]{2,1,0:T(8,128)(2,1)}) %all-gather.21.cloned.1.call-update) | async-done | bytes 3145744 | tf_op jit(solution)/shard_map/all_gather | solution.py:211
  284.9 2.7 multiply_reduce_fusion.10
  288.8 17.2 %gather_rows.5 = bf16[32,32,768]{2,1,0:T(8,128)(2,1)} custom-call(bf16[32,768]{1,0:T(8,128)(2,1)} %multiply_convert_fusion.5.x_ref), custom_call_target="tpu_custom_call" | custom-call | tf_op jit(solution)/shard_map/gather_rows/pallas_call | solution.py:112
  306.0 4.1 fusion.179
  310.2 2.0 copy-done.8
  312.2 1.7 exponential_reduce_fusion
  315.9 12.5 %gather_rows.6 = f32[32,32,128]{2,1,0:T(8,128)} custom-call(f32[32,128]{1,0:T(8,128)} %reshape.419.x_ref), custom_call_target="tpu_custom_call" | custom-call | tf_op jit(solution)/shard_map/gather_rows/pallas_call | solution.py:112
  328.4 2.0 reshape.420
  330.4 3.1 slice_reduce_fusion.1
  334.7 7.8 fusion.65
  343.2 99.5 %reduce-scatter.6.cloned.1.call-done = f32[32,768]{1,0:T(8,128)} async-done(((f32[1024,768]{1,0:T(8,128)}), f32[32,768]{1,0:T(8,128)}) %reduce-scatter.6.cloned.1.call-update) | async-done | bytes 98320 | tf_op jit(solution)/shard_map/reduce_scatter | solution.py:353
  442.7 1.6 multiply_reduce_fusion.6
  444.8 1.6 fusion.162
  446.5 1.7 convolution_bitcast_fusion.3
  448.2 1.6 convolution_bitcast_fusion.4
  451.8 5.6 multiply_reduce_fusion.7
  459.4 1.6 constant_dynamic-update-slice_fusion.3
  462.9 2.8 fusion.124
  470.7 2.2 convert_reduce_fusion.1
  479.5 1.8 copy.194
  481.3 2.7 copy.193
  488.9 2.2 convert_reduce_fusion.4
  491.1 1.6 copy.195
  496.8 9.2 fusion.164
  506.1 2.7 copy.196
  511.9 3.6 all-to-all-start.1
  516.4 2.0 fusion.119
  518.4 8.7 all-to-all-done.1
  527.1 3.3 all-to-all-start.3
  535.2 2.8 fusion.181
  539.5 4.6 all-to-all-start.2
  544.2 8.8 fusion.19
  553.0 2.1 fusion.18
  555.2 6.5 all-to-all-done.2
  561.7 2.7 all-to-all-start.4
  565.0 1.6 copy.215
  572.8 7.2 multiply_reduce_fusion.2
  581.9 2.4 multiply_reduce_fusion.5
  584.3 81.7 %reduce-scatter.8.cloned.1.call-done = f32[24,768]{1,0:T(8,128)} async-done(((f32[768,768]{1,0:T(8,128)}), f32[24,768]{1,0:T(8,128)}) %reduce-scatter.8.cloned.1.call-update) | async-done | bytes 73744 | tf_op jit(solution)/shard_map/reduce_scatter | solution.py:396
  667.5 2.0 convert_bitcast_fusion
  669.5 9.8 %copy.203 = f32[32,1024,24]{2,1,0:T(8,128)} copy(f32[32,1024,24]{1,2,0:T(8,128)} %convert_bitcast_fusion) | data formatting | bytes 6291456 | tf_op jit(solution)/shard_map/convert_element_type | solution.py:476
  679.4 180.8 %scatter_custom_fusion = f32[32000,24]{1,0:T(8,128)} fusion(s32[32768]{0:T(1024)} %bitcast.321, f32[32768,24]{1,0:T(8,128)} %bitcast.294, f32[]{:T(128)} %constant.33.clone.1), kind=kCustom, calls=%fused_computation.3 | custom fusion | flops 786432 | bytes 3072512 | tf_op jit(solution)/shard_map/scatter-add | solution.py:475
  860.2 11.0 %copy.205 = f32[32000,24]{0,1:T(8,128)} copy(f32[32000,24]{1,0:T(8,128)} %scatter_custom_fusion) | data formatting | bytes 6144000 | tf_op jit(solution)/shard_map/scatter-add | solution.py:475
  871.2 8.5 multiply_reduce_fusion
  879.8 1.7 multiply_reduce_fusion.4
  886.1 12.8 %gather_rows.7 = f32[32,24,128]{2,1,0:T(8,128)} custom-call(f32[24,128]{1,0:T(8,128)} %pad_bitcast_fusion.x_ref), custom_call_target="tpu_custom_call" | custom-call | tf_op jit(solution)/shard_map/gather_rows/pallas_call | solution.py:112
  907.1 8.3 multiply_add_fusion.2
  915.4 7.6 multiply_add_fusion
  (384 shorter events, 89.6 us)
Async XLA Ops:
  7.2 219.1 %all-gather.15.cloned.1.call-start = ((), (), s32[]{:S(2)}) async-start(), calls=%async_computation.12 | async-start | bytes 3852288 | tf_op jit(solution)/shard_map/all_gather | solution.py:208
  8.9 246.2 %all-gather.17.cloned.1.call-start = ((), (), s32[]{:S(2)}) async-start(), calls=%async_computation.13 | async-start | bytes 1216512 | tf_op jit(solution)/shard_map/all_gather | solution.py:209
  10.4 247.0 %all-gather.19.cloned.1.call-start = ((), (), s32[]{:S(2)}) async-start(), calls=%async_computation.14 | async-start | bytes 6488064 | tf_op jit(solution)/shard_map/all_gather | solution.py:210
  14.3 7.3 copy-start.67
  14.3 7.4 copy-start.85
  14.3 7.6 copy-start.73
  38.4 127.8 %copy-start.21 = (s32[4,8,16,128]{3,1,2,0:T(8,128)}, s32[4,8,16,128]{3,1,2,0:T(8,128)S(1)}, u32[]{:S(2)}) copy-start(s32[4,8,16,128]{3,1,2,0:T(8,128)S(1)} %copy.240) | copy-start | bytes 786436
  161.1 63.2 %all-to-all-start = ((bf16[32,24,1024]{2,1,0:T(8,128)(2,1)}), bf16[32,24,1024]{2,1,0:T(8,128)(2,1)S(1)}, u32[]{:S(2)}, u32[]{:S(2)}) async-start(bf16[32,24,1024]{2,1,0:T(8,128)(2,1)} %select_bitcast_fusion), calls=%async_computation | async-start | bytes 3145728 | tf_op jit(solution)/shard_map/all_to_all | solution.py:215
  164.4 120.4 %all-gather.21.cloned.1.call-start = ((), (), s32[]{:S(2)}) async-start(), calls=%async_computation.15 | async-start | bytes 3244032 | tf_op jit(solution)/shard_map/all_gather | solution.py:211
  164.5 4.1 collective-permute-start
  165.5 277.2 %reduce-scatter.6.cloned.1.call-start = ((), (), s32[]{:S(2)}) async-start(), calls=%async_computation.8 | async-start | bytes 3244032 | tf_op jit(solution)/shard_map/reduce_scatter | solution.py:353
  166.1 66.5 %copy-start.76 = (f32[12]{0:T(128)}, f32[12]{0:T(128)S(1)}, u32[]{:S(2)}) copy-start(f32[12]{0:T(128)S(1)} %slice.267) | copy-start | bytes 148
  166.2 167.9 %copy-start.64 = (s32[1024]{0:T(1024)}, s32[1024]{0:T(1024)S(1)}, u32[]{:S(2)}) copy-start(s32[1024]{0:T(1024)S(1)} %eq.53) | copy-start | bytes 12292
  168.0 77.8 %copy-start.59 = (s32[16]{0:T(128)}, s32[16]{0:T(128)S(1)}, u32[]{:S(2)}) copy-start(s32[16]{0:T(128)S(1)} %get-tuple-element.202) | copy-start | bytes 196
  168.0 82.8 %copy-start.57 = (s32[16]{0:T(128)}, s32[16]{0:T(128)S(1)}, u32[]{:S(2)}) copy-start(s32[16]{0:T(128)S(1)} %get-tuple-element.201) | copy-start | bytes 196
  168.0 58.3 %copy-start.55 = (f32[768]{0:T(1024)}, f32[768]{0:T(1024)S(1)}, u32[]{:S(2)}) copy-start(f32[768]{0:T(1024)S(1)} %get-tuple-element.194) | copy-start | bytes 9220
  225.3 7.3 copy-start.53
  239.7 2.5 collective-permute-start.2
  242.1 1.7 collective-permute-start.1
  242.2 1.3 collective-permute-start.3
  245.4 1.5 collective-permute-start.5
  246.7 1.2 collective-permute-start.4
  250.5 1.5 collective-permute-start.6
  288.1 17.9 %copy-start.68 = (f32[32]{0:T(128)}, f32[32]{0:T(128)S(1)}, u32[]{:S(2)}) copy-start(f32[32]{0:T(128)S(1)} %get-tuple-element.206) | copy-start | bytes 388
  342.5 100.2 %copy-start.69 = (f32[32]{0:T(128)S(1)}, f32[32]{0:T(128)}, u32[]{:S(2)}) copy-start(f32[32]{0:T(128)} %copy-done.68) | copy-start | bytes 388
  342.5 102.2 %copy-start.78 = (f32[32]{0:T(128)S(1)}, f32[32]{0:T(128)}, u32[]{:S(2)}) copy-start(f32[32]{0:T(128)} %get-tuple-element.205) | copy-start | bytes 388
  342.6 163.5 %all-gather.11.cloned.1.call-start = ((), (), s32[]{:S(2)}) async-start(), calls=%async_computation.10 | async-start | bytes 1622016 | tf_op jit(solution)/shard_map/all_gather | solution.py:370
  343.1 238.7 %all-gather.13.cloned.1.call-start = ((), (), s32[]{:S(2)}) async-start(), calls=%async_computation.11 | async-start | bytes 1622016 | tf_op jit(solution)/shard_map/all_gather | solution.py:371
  446.4 219.6 %reduce-scatter.8.cloned.1.call-start = ((), (), s32[]{:S(2)}) async-start(), calls=%async_computation.9 | async-start | bytes 2433024 | tf_op jit(solution)/shard_map/reduce_scatter | solution.py:396
  450.6 10.9 %collective-permute-start.8 = (f32[2,16,12,64]{3,1,2,0:T(8,128)}, f32[2,16,12,64]{3,1,2,0:T(8,128)}, u32[]{:S(2)}, u32[]{:S(2)}) collective-permute-start(f32[2,16,12,64]{3,1,2,0:T(8,128)} %pad_maximum_fusion.6), channel_id=1, source_target_pairs={{0,16},{16,0},{1,17},{17,1},{2,18},{18,2},{3,19},{19,3},{4,20},{20... | collective-permute-start | bytes 294920 | tf_op jit(solution)/shard_map/ppermute | solution.py:127
  461.0 5.7 collective-permute-start.7
  462.9 3.0 collective-permute-start.9
  465.8 414.0 %reduce-scatter.10.cloned.1.call-start = ((), (), s32[]{:S(2)}) async-start(), calls=%async_computation.16 | async-start | bytes 7704576
  476.1 7.9 collective-permute-start.11
  479.5 7.3 copy-start.58
  481.2 15.6 %copy-start.4 = (bf16[768,1024]{1,0:T(8,128)(2,1)S(1)}, bf16[768,1024]{1,0:T(8,128)(2,1)}, u32[]{:S(2)}) copy-start(bf16[768,1024]{1,0:T(8,128)(2,1)} %copy-done.3) | copy-start | bytes 4718596
  483.9 8.8 collective-permute-start.10
  511.9 15.1 %all-to-all-start.1 = ((bf16[32,2,2048]{2,1,0:T(2,128)(2,1)}), bf16[32,2,2048]{2,1,0:T(2,128)(2,1)S(1)}, u32[]{:S(2)}, u32[]{:S(2)}) async-start(bf16[32,2,2048]{2,1,0:T(2,128)(2,1)} %reshape.475), calls=%async_computation.3 | async-start | bytes 524288 | tf_op jit(solution)/shard_map/all_to_all | solution.py:376
  527.1 12.4 %all-to-all-start.3 = ((bf16[32,2,1024]{2,1,0:T(2,128)(2,1)}), bf16[32,2,1024]{2,1,0:T(2,128)(2,1)}, u32[]{:S(2)}, u32[]{:S(2)}) async-start(bf16[32,2,1024]{2,1,0:T(2,128)(2,1)} %reshape.477), calls=%async_computation.5 | async-start | bytes 262144 | tf_op jit(solution)/shard_map/all_to_all | solution.py:372
  531.5 12.6 %copy-start.54 = (f32[1024]{0:T(1024)S(1)}, f32[1024]{0:T(1024)}, u32[]{:S(2)}) copy-start(f32[1024]{0:T(1024)} %copy-done.53) | copy-start | bytes 12292
  531.5 12.7 %copy-start.56 = (f32[768]{0:T(1024)S(1)}, f32[768]{0:T(1024)}, u32[]{:S(2)}) copy-start(f32[768]{0:T(1024)} %copy-done.55) | copy-start | bytes 9220
  539.5 22.1 %all-to-all-start.2 = ((f32[32,24,128]{2,1,0:T(8,128)}), f32[32,24,128]{2,1,0:T(8,128)S(1)}, u32[]{:S(2)}, u32[]{:S(2)}) async-start(f32[32,24,128]{2,1,0:T(8,128)} %fusion.181), calls=%async_computation.4 | async-start | bytes 786432 | tf_op jit(solution)/shard_map/all_to_all | solution.py:384
  544.2 8.8 copy-start.2
  544.2 8.8 copy-start.61
  555.2 9.2 copy-start.83
  555.2 17.6 %copy-start.17 = (bf16[32,32,768]{2,1,0:T(8,128)(2,1)S(1)}, bf16[32,32,768]{2,1,0:T(8,128)(2,1)}, u32[]{:S(2)}) copy-start(bf16[32,32,768]{2,1,0:T(8,128)(2,1)} %gather_rows.5) | copy-start | bytes 4718596
  561.7 105.8 %all-to-all-start.4 = ((bf16[32,24,1024]{2,1,0:T(8,128)(2,1)}), bf16[32,24,1024]{2,1,0:T(8,128)(2,1)S(1)}, u32[]{:S(2)}, u32[]{:S(2)}) async-start(bf16[32,24,1024]{2,1,0:T(8,128)(2,1)} %bitcast.76), calls=%async_computation.6 | async-start | bytes 3145728 | tf_op jit(solution)/shard_map/all_to_all | solution.py:474
  871.2 14.2 %copy-start.62 = (f32[768]{0:T(1024)S(1)}, f32[768]{0:T(1024)}, u32[]{:S(2)}) copy-start(f32[768]{0:T(1024)} %get-tuple-element.127) | copy-start | bytes 9220
  871.2 14.2 %copy-start.65 = (f32[768]{0:T(1024)S(1)}, f32[768]{0:T(1024)}, u32[]{:S(2)}) copy-start(f32[768]{0:T(1024)} %get-tuple-element.129) | copy-start | bytes 9220
  871.2 14.2 %copy-start.72 = (f32[768]{0:T(1024)S(1)}, f32[768]{0:T(1024)}, u32[]{:S(2)}) copy-start(f32[768]{0:T(1024)} %get-tuple-element.116) | copy-start | bytes 9220
  871.2 14.2 %copy-start.77 = (f32[12]{0:T(128)S(1)}, f32[12]{0:T(128)}, u32[]{:S(2)}) copy-start(f32[12]{0:T(128)} %get-tuple-element.154) | copy-start | bytes 148
  879.8 25.3 %copy-start.20 = (f32[1,24,4096]{2,1,0:T(8,128)S(1)}, f32[1,24,4096]{2,1,0:T(8,128)}, u32[]{:S(2)}) copy-start(f32[1,24,4096]{2,1,0:T(8,128)} %param.35) | copy-start | bytes 1179652
  879.8 25.3 %copy-start.42 = (f32[1,24,4096]{2,1,0:T(8,128)S(1)}, f32[1,24,4096]{2,1,0:T(8,128)}, u32[]{:S(2)}) copy-start(f32[1,24,4096]{2,1,0:T(8,128)} %param.37) | copy-start | bytes 1179652
  879.8 25.3 %copy-start.43 = (f32[1,24,4096]{2,1,0:T(8,128)S(1)}, f32[1,24,4096]{2,1,0:T(8,128)}, u32[]{:S(2)}) copy-start(f32[1,24,4096]{2,1,0:T(8,128)} %param.36) | copy-start | bytes 1179652
  907.1 8.3 copy-start.12
  907.1 8.3 copy-start.13
  915.4 7.7 copy-start.27
  915.4 7.7 copy-start.28
  915.4 7.7 copy-start.46
  915.4 7.7 copy-start.47
  915.4 8.6 copy-start.44
  915.4 8.6 copy-start.45
  915.4 8.6 copy-start.50
  915.4 8.6 copy-start.51
  (48 other events, 176.6 us)
Sparse Core Ops, SparseCore 0:
  11.4 63.6 all-gather.14
  78.6 52.5 all-gather.16
  134.7 88.8 all-gather.18
  226.8 57.9 all-gather.20
  342.7 99.9 reduce-scatter.5
  446.0 54.0 all-gather.10
  503.5 57.5 all-gather.12
  566.9 99.0 reduce-scatter.7
  671.7 120.1 reduce-scatter.9
